TPU v7x, 768 devices: a whole 4x8x12 slice. The times are simulated.
768 devices in a mesh: group: 48 (over z, x), fsdp: 4 (over y_hi, core), tensor: 4 (over y_lo).
Axes of the slice: x: 4, y: 8 (y_hi: 2, y_lo: 4; y = y_hi * 4 + y_lo), z: 12, core: 2. Of those that a mesh axis runs over, the one named last changes fastest.
Arguments:
- tokens: bfloat16 [24576, 8192], P(('group', 'fsdp')), may hold values from -6 to 6
- cotangent: bfloat16 [24576, 512], P(('group', 'fsdp'), 'tensor'), may hold values from -0.0390625 to 0.0390625
- weight: bfloat16 [8192, 512], P('fsdp', 'tensor'), may hold values from -0.0625 to 0.0625
- moment_one: float32 [8192, 512], P('fsdp', 'tensor'), may hold values from -4 to 4
- moment_two: float32 [8192, 512], P('fsdp', 'tensor'), may hold values from 0.003 to 0.3
- hidden: bfloat16 [4, 12288, 8192], P(None, 'group', ('fsdp', 'tensor')), may hold values from -6 to 6
- queries: bfloat16 [4, 12288, 4096], P(None, ('group', 'fsdp', 'tensor')), may hold values from -145 to 145
- new_keys: bfloat16 [4, 12288, 512], P(None, ('group', 'fsdp', 'tensor')), may hold values from -4 to 4
- key_cache: bfloat16 [12288, 32, 512], P(('group', 'fsdp', 'tensor')), may hold values from -4 to 4
- value_cache: bfloat16 [12288, 32, 512], P(('group', 'fsdp', 'tensor')), may hold values from -6 to 6
- lengths: int32 [12288], P(('group', 'fsdp', 'tensor')), may hold values from 2 to 32
Outputs:
- new_weight: bfloat16 [8192, 512], P('fsdp', 'tensor')
- new_moment_one: float32 [8192, 512], P('fsdp', 'tensor')
- new_moment_two: float32 [8192, 512], P('fsdp', 'tensor')
- attention: bfloat16 [4, 12288, 4096], P(None, ('group', 'fsdp', 'tensor'))
All inputs are finite; a program needn't handle non-finite values.
Results may differ from a plain program's by a relative error of at most 0.007.
Values may be sent and summed in bfloat16 or wider, within the bound.
No kernel may reach another device: no remote copies, remote signals or barrier semaphores. Data moves between devices by JAX's collectives and lax.ppermute only.
A program may use at most 64 MiB of HBM per device.

v0:
```python
import jax
import jax.numpy as jnp
from jax import lax
from jax.sharding import Mesh
from jax.sharding import PartitionSpec as P

HEAD_DIM = 128
GROUP_HEADS = 8
KV_HEADS = 4
STEPS = 4
ADAM_STEP = 10
GROUP = ("group_0", "group_1")
GROUP_FSDP = ("group_0", "group_1", "fsdp")
GROUP_FSDP_TENSOR = ("group_0", "group_1", "fsdp", "tensor")


learn_rate = 0.001
beta_one = 0.9
beta_two = 0.95
epsilon = 1e-08
decay_rate = 0.1
masked_score = -1e30


def filled_up(lines, peers):
    spare = -len(lines) % peers
    return jnp.pad(lines, [(0, spare)] + [(0, 0)] * (lines.ndim - 1))


def own_block(parts, axes, order):
    inside = parts.shape[1:]
    parts = parts.reshape(*(lax.axis_size(a) for a in axes), *inside)
    parts = jnp.moveaxis(parts, order, range(len(axes))).reshape(-1, *inside)
    for k in order:
        parts = lax.psum_scatter(parts, axes[k], scatter_dimension=0, tiled=True)
    return parts[0]


def stacked_from(shard, axes, order):
    parts = shard[None]
    for k in order:
        parts = lax.all_gather(parts, axes[k], axis=0, tiled=True)
    carried = [lax.axis_size(axes[k]) for k in reversed(order)]
    parts = parts.reshape(*carried, *shard.shape)
    turned = sorted(range(len(order)), key=lambda place: order[len(order) - 1 - place])
    return parts.transpose(*turned, *range(len(order), parts.ndim)).reshape(-1, *shard.shape)


def sum_at_once(shard, axes):
    peers, count = (lax.axis_size(axes), len(axes))
    lines = shard.reshape(-1, *shard.shape[1:][-1:])
    parts = filled_up(lines, peers * count).reshape(count, peers, -1, *lines.shape[1:])
    finished = []
    for initial in range(count):
        order = [(initial + k) % count for k in range(count)]
        own = own_block(parts[initial], axes, order)
        finished.append(stacked_from(own, axes, order[::-1]).reshape(-1, *lines.shape[1:]))
    return jnp.concatenate(finished)[: len(lines)].reshape(shard.shape)


def cut_along(shard, dim, peers):
    shape = shard.shape
    parts = shard.reshape(*shape[:dim], peers, shape[dim] // peers, *shape[dim + 1 :])
    return jnp.moveaxis(parts, dim, 0)


def sent_and_summed(shard, axis, dim):
    peers = lax.axis_size(axis)
    parts = lax.all_to_all(cut_along(shard, dim, peers), axis, 0, 0, tiled=True)
    return jnp.sum(parts, axis=0)


def apply_adamw(gradient, weight, moment_one, moment_two):
    first_new = beta_one * moment_one + (1.0 - beta_one) * gradient
    second_new = beta_two * moment_two + (1.0 - beta_two) * gradient * gradient
    first_hat = first_new / (1.0 - beta_one**ADAM_STEP)
    second_hat = second_new / (1.0 - beta_two**ADAM_STEP)
    stepped = weight.astype(jnp.float32) * (
        1.0 - learn_rate * decay_rate
    ) - learn_rate * first_hat / (jnp.sqrt(second_hat) + epsilon)
    return (stepped.astype(jnp.bfloat16), first_new, second_new)


def attend(queries, new_keys, fresh_values, key_cache, value_cache, lengths):
    row_total = lengths.shape[0]
    cache_len = key_cache.shape[1]
    query_b = queries.reshape(STEPS, row_total, KV_HEADS, GROUP_HEADS, HEAD_DIM)
    cached_keys = key_cache.reshape(row_total, cache_len, KV_HEADS, HEAD_DIM)
    cached_values = value_cache.reshape(row_total, cache_len, KV_HEADS, HEAD_DIM)
    fresh_keys = new_keys.reshape(STEPS, row_total, KV_HEADS, HEAD_DIM)
    fresh_vals = fresh_values.reshape(STEPS, row_total, KV_HEADS, HEAD_DIM)
    score_scale = HEAD_DIM ** (-0.5)
    cached_scores = (
        jnp.einsum("tnhjd,nphd->nhjtp", query_b, cached_keys, preferred_element_type=jnp.float32)
        * score_scale
    )
    fresh_scores = (
        jnp.einsum("tnhjd,snhd->nhjts", query_b, fresh_keys, preferred_element_type=jnp.float32)
        * score_scale
    )
    cached_valid = jnp.arange(cache_len, dtype=jnp.int32)[None, :] < lengths[:, None]
    fresh_valid = (
        jnp.arange(STEPS, dtype=jnp.int32)[None, :] <= jnp.arange(STEPS, dtype=jnp.int32)[:, None]
    )
    cached_scores = jnp.where(cached_valid[:, None, None, None, :], cached_scores, masked_score)
    fresh_scores = jnp.where(fresh_valid[None, None, None, :, :], fresh_scores, masked_score)
    highest = jnp.maximum(jnp.max(cached_scores, axis=-1), jnp.max(fresh_scores, axis=-1))[
        ..., None
    ]
    cached_exp = jnp.exp(cached_scores - highest)
    fresh_exp = jnp.exp(fresh_scores - highest)
    denominator = jnp.sum(cached_exp, axis=-1, keepdims=True) + jnp.sum(
        fresh_exp, axis=-1, keepdims=True
    )
    cached_probs = (cached_exp / denominator).astype(jnp.bfloat16)
    fresh_probs = (fresh_exp / denominator).astype(jnp.bfloat16)
    result = jnp.einsum(
        "nhjtp,nphd->tnhjd", cached_probs, cached_values, preferred_element_type=jnp.float32
    )
    result = result + jnp.einsum(
        "nhjts,snhd->tnhjd", fresh_probs, fresh_vals, preferred_element_type=jnp.float32
    )
    return result.reshape(STEPS, row_total, queries.shape[2]).astype(jnp.bfloat16)


def per_device(
    tokens,
    cotangent,
    weight,
    moment_one,
    moment_two,
    hidden,
    queries,
    new_keys,
    key_cache,
    value_cache,
    lengths,
):
    contract_rows = (((0,), (0,)), ((), ()))
    token_cols = lax.all_to_all(tokens, "fsdp", split_axis=1, concat_axis=0, tiled=True)
    upstream = lax.all_gather(cotangent, "fsdp", axis=0, tiled=True)
    partial_grad = lax.dot_general(
        token_cols, upstream, contract_rows, preferred_element_type=jnp.float32
    )
    gradient = sum_at_once(partial_grad, GROUP)
    new_weight, first_new, second_new = apply_adamw(gradient, weight, moment_one, moment_two)
    weight_rows = lax.all_to_all(new_weight, "tensor", split_axis=0, concat_axis=1, tiled=True)
    local_rows = lengths.shape[0]
    width_kv = weight_rows.shape[1]
    product = jnp.einsum("snc,ck->nsk", hidden, weight_rows, preferred_element_type=jnp.float32)
    summed = sent_and_summed(
        product.reshape(local_rows * lax.axis_size(("fsdp", "tensor")), STEPS * width_kv),
        ("fsdp", "tensor"),
        0,
    )
    fresh = jnp.transpose(summed.reshape(local_rows, STEPS, width_kv), (1, 0, 2)).astype(
        jnp.bfloat16
    )
    attention = attend(queries, new_keys, fresh, key_cache, value_cache, lengths)
    return (new_weight, first_new, second_new, attention)


def solution(mesh):
    split = Mesh(
        mesh.devices.reshape(12, 4, mesh.shape["fsdp"], mesh.shape["tensor"]),
        ("group_0", "group_1", "fsdp", "tensor"),
    )
    return jax.shard_map(
        per_device,
        mesh=split,
        in_specs=(
            P(GROUP_FSDP, None),
            P(GROUP_FSDP, "tensor"),
            P("fsdp", "tensor"),
            P("fsdp", "tensor"),
            P("fsdp", "tensor"),
            P(None, GROUP, ("fsdp", "tensor")),
            P(None, GROUP_FSDP_TENSOR, None),
            P(None, GROUP_FSDP_TENSOR, None),
            P(GROUP_FSDP_TENSOR, None, None),
            P(GROUP_FSDP_TENSOR, None, None),
            P(GROUP_FSDP_TENSOR),
        ),
        out_specs=(
            P("fsdp", "tensor"),
            P("fsdp", "tensor"),
            P("fsdp", "tensor"),
            P(None, GROUP_FSDP_TENSOR, None),
        ),
        check_vma=False,
    )
```

profile of v0, /device:TPU:9, one launch (start us, length us, event | category | flops | bytes accessed | tf_op | source)
XLA Modules:
  0.0 387.3 jit_solution(17043139332527991616)
XLA Ops:
  7.2 4.1 %copy.43 = bf16[128,8192]{0,1:T(8,128)(2,1)} copy(bf16[128,8192]{1,0:T(8,128)(2,1)} %param.11) | data formatting | bytes 4194304 | tf_op args[0]
  11.3 7.0 %all-to-all-start = ((bf16[128,4,2048]{0,2,1:T(8,128)(2,1)}), bf16[128,4,2048]{0,2,1:T(8,128)(2,1)S(1)}, u32[]{:S(2)}, u32[]{:S(2)}) async-start(bf16[128,4,2048]{0,2,1:T(8,128)(2,1)} %bitcast.56), calls=%async_computation | async-start | bytes 4194304 | tf_op jit(solution)/shard_map/all_to_all | solution.py:140
  18.3 54.1 %all_gather.15 = bf16[512,128]{1,0:T(8,128)(2,1)S(1)} all-gather(bf16[128,128]{1,0:T(8,128)(2,1)S(1)} %copy-done.9), channel_id=1, replica_groups=mesh['group_0'=12,'group_1'=4,'fsdp'=4,'tensor'=4] {'fsdp'}, dimensions={0}, use_global_device_ids=true | all-gather | bytes 163840 | tf_op jit(solution)/shard_map/all_gather | solution.py:141
  72.5 1.3 copy-done.1
  73.8 2.9 copy.44
  76.7 0.7 fusion.23
  77.5 0.9 reshape_reshape_squeeze.3
  78.5 0.9 copy.45
  79.5 51.7 %reduce-scatter.9.cloned.1.call-done = f32[4,22,128]{2,1,0:T(8,128)} async-done(((f32[48,22,128]{2,1,0:T(8,128)}), f32[4,22,128]{2,1,0:T(8,128)}) %reduce-scatter.9.cloned.1.call-update) | async-done | bytes 45072 | tf_op jit(solution)/shard_map/reduce_scatter | solution.py:35
  131.2 36.9 %reduce-scatter.11.cloned.1.call-done = f32[12,22,128]{2,1,0:T(8,128)} async-done(((f32[48,22,128]{2,1,0:T(8,128)}), f32[12,22,128]{2,1,0:T(8,128)}) %reduce-scatter.11.cloned.1.call-update) | async-done | bytes 135184 | tf_op jit(solution)/shard_map/reduce_scatter | solution.py:35
  168.1 31.2 %reduce-scatter.13.cloned.1.call-done = f32[1,22,128]{2,1,0:T(8,128)} async-done(((f32[4,22,128]{2,1,0:T(8,128)}), f32[1,22,128]{2,1,0:T(8,128)}) %reduce-scatter.13.cloned.1.call-update) | async-done | bytes 11280
  199.3 9.2 %all_gather.16 = f32[4,22,128]{2,1,0:T(8,128)S(1)} all-gather(f32[1,22,128]{2,1,0:T(8,128)} %reduce-scatter.13.cloned.1.call-done), channel_id=1, replica_groups=mesh['group_0'=12,'group_1'=4,'fsdp'=4,'tensor'=4] {'group_1'}, dimensions={0}, use_global_device_ids=true | all-gather | bytes 56320 | tf_op jit(solution)/shard_map/all_gather | solution.py:42
  208.5 22.7 %all_gather.17 = f32[48,22,128]{2,1,0:T(8,128)S(1)} all-gather(f32[4,22,128]{2,1,0:T(8,128)S(1)} %all_gather.16), channel_id=1, replica_groups=mesh['group_0'=12,'group_1'=4,'fsdp'=4,'tensor'=4] {'group_0'}, dimensions={0}, use_global_device_ids=true | all-gather | bytes 585728 | tf_op jit(solution)/shard_map/all_gather | solution.py:42
  231.2 22.5 %reduce-scatter.15.cloned.1.call-done = f32[1,22,128]{2,1,0:T(8,128)} async-done(((f32[12,22,128]{2,1,0:T(8,128)}), f32[1,22,128]{2,1,0:T(8,128)}) %reduce-scatter.15.cloned.1.call-update) | async-done | bytes 11280
  253.7 16.6 %all_gather.18 = f32[12,22,128]{2,1,0:T(8,128)S(1)} all-gather(f32[1,22,128]{2,1,0:T(8,128)} %reduce-scatter.15.cloned.1.call-done), channel_id=1, replica_groups=mesh['group_0'=12,'group_1'=4,'fsdp'=4,'tensor'=4] {'group_0'}, dimensions={0}, use_global_device_ids=true | all-gather | bytes 146432 | tf_op jit(solution)/shard_map/all_gather | solution.py:42
  270.3 10.9 %all_gather.19 = f32[48,22,128]{2,1,0:T(8,128)S(1)} all-gather(f32[12,22,128]{2,1,0:T(8,128)S(1)} %all_gather.18), channel_id=1, replica_groups=mesh['group_0'=12,'group_1'=4,'fsdp'=4,'tensor'=4] {'group_1'}, dimensions={0}, use_global_device_ids=true | all-gather | bytes 675840 | tf_op jit(solution)/shard_map/all_gather | solution.py:42
  281.4 3.6 subtract_convert_fusion
  285.2 12.0 %all_to_all.43 = bf16[4,512,128]{1,2,0:T(8,128)(2,1)S(1)} all-to-all(bf16[4,512,128]{1,2,0:T(8,128)(2,1)S(1)} %copy.52), channel_id=1, replica_groups=mesh['group_0'=12,'group_1'=4,'fsdp'=4,'tensor'=4] {'tensor'}, dimensions={0} | all-to-all | bytes 1048576 | tf_op jit(solution)/shard_map/all_to_all | solution.py:147
  297.2 0.7 convolution_bitcast_fusion
  297.9 2.0 copy.53
  299.9 3.7 reshape_reshape.7
  303.6 24.0 %all-to-all-start.2 = ((f32[16,16,2048]{2,1,0:T(8,128)}), f32[16,16,2048]{2,1,0:T(8,128)S(1)}, u32[]{:S(2)}, u32[]{:S(2)}) async-start(f32[16,16,2048]{2,1,0:T(8,128)} %reshape_reshape.7), calls=%async_computation.4 | async-start | bytes 4194304 | tf_op jit(solution)/shard_map/all_to_all | solution.py:69
  327.6 1.9 copy.65
  329.5 2.0 reshape.86
  331.5 1.9 reshape.89
  333.5 3.5 fusion.22
  337.1 1.9 fusion.21
  339.5 0.8 fusion.7
  340.3 36.6 %all-to-all-done.2 = f32[16,16,2048]{2,1,0:T(8,128)S(1)} async-done(((f32[16,16,2048]{2,1,0:T(8,128)}), f32[16,16,2048]{2,1,0:T(8,128)S(1)}, u32[]{:S(2)}, u32[]{:S(2)}) %all-to-all-start.2) | async-done | bytes 2097184 | tf_op jit(solution)/shard_map/all_to_all | solution.py:69
  377.0 1.6 convolution_bitcast_fusion.1
  378.7 1.0 fusion.3
  379.8 1.0 convert_element_type.37
  (45 shorter events, 1.6 us)
Async XLA Ops:
  7.2 290.0 %copy-start = (bf16[4,256,512]{2,1,0:T(8,128)(2,1)S(1)}, bf16[4,256,512]{2,1,0:T(8,128)(2,1)}, u32[]{:S(2)}) copy-start(bf16[4,256,512]{2,1,0:T(8,128)(2,1)} %param.16) | copy-start | bytes 3145732
  11.3 7.0 %copy-start.9 = (bf16[128,128]{1,0:T(8,128)(2,1)S(1)}, bf16[128,128]{1,0:T(8,128)(2,1)}, u32[]{:S(2)}) copy-start(bf16[128,128]{1,0:T(8,128)(2,1)} %param.12) | copy-start | bytes 98308
  11.3 61.1 %all-to-all-start = ((bf16[128,4,2048]{0,2,1:T(8,128)(2,1)}), bf16[128,4,2048]{0,2,1:T(8,128)(2,1)S(1)}, u32[]{:S(2)}, u32[]{:S(2)}) async-start(bf16[128,4,2048]{0,2,1:T(8,128)(2,1)} %bitcast.56), calls=%async_computation | async-start | bytes 4194304 | tf_op jit(solution)/shard_map/all_to_all | solution.py:140
  18.3 112.8 %reduce-scatter.9.cloned.1.call-start = ((), (), s32[]{:S(2)}) async-start(), calls=%async_computation.7 | async-start | bytes 638976 | tf_op jit(solution)/shard_map/reduce_scatter | solution.py:35
  72.5 1.3 copy-start.1
  78.4 89.7 %reduce-scatter.11.cloned.1.call-start = ((), (), s32[]{:S(2)}) async-start(), calls=%async_computation.8 | async-start | bytes 737280 | tf_op jit(solution)/shard_map/reduce_scatter | solution.py:35
  79.4 119.9 %reduce-scatter.13.cloned.1.call-start = ((), (), s32[]{:S(2)}) async-start(), calls=%async_computation.9 | async-start | bytes 61440
  131.1 122.6 %reduce-scatter.15.cloned.1.call-start = ((), (), s32[]{:S(2)}) async-start(), calls=%async_computation.10 | async-start | bytes 159744
  231.2 50.2 %copy-start.5 = (bf16[2048,128]{1,0:T(8,128)(2,1)S(1)}, bf16[2048,128]{1,0:T(8,128)(2,1)}, u32[]{:S(2)}) copy-start(bf16[2048,128]{1,0:T(8,128)(2,1)} %param.13) | copy-start | bytes 1572868
  285.0 12.2 %copy-start.2 = (bf16[2048,128]{1,0:T(8,128)(2,1)}, bf16[2048,128]{1,0:T(8,128)(2,1)S(1)}, u32[]{:S(2)}) copy-start(bf16[2048,128]{1,0:T(8,128)(2,1)S(1)} %get-tuple-element.4) | copy-start | bytes 1572868
  303.6 25.9 %copy-start.8 = (bf16[4,16,512]{2,1,0:T(8,128)(2,1)S(1)}, bf16[4,16,512]{2,1,0:T(8,128)(2,1)}, u32[]{:S(2)}) copy-start(bf16[4,16,512]{2,1,0:T(8,128)(2,1)} %param.18) | copy-start | bytes 196612
  303.6 73.3 %all-to-all-start.2 = ((f32[16,16,2048]{2,1,0:T(8,128)}), f32[16,16,2048]{2,1,0:T(8,128)S(1)}, u32[]{:S(2)}, u32[]{:S(2)}) async-start(f32[16,16,2048]{2,1,0:T(8,128)} %reshape_reshape.7), calls=%async_computation.4 | async-start | bytes 4194304 | tf_op jit(solution)/shard_map/all_to_all | solution.py:69
  327.6 5.9 %copy-start.10 = (s32[16]{0:T(128)S(1)}, s32[16]{0:T(128)}, u32[]{:S(2)}) copy-start(s32[16]{0:T(128)} %param.21) | copy-start | bytes 196
  337.0 2.4 copy-start.6
  339.0 1.3 copy-start.3
  377.0 1.7 copy-start.4
  377.0 1.7 copy-start.7
Sparse Core Ops, SparseCore 0:
  78.5 52.5 reduce-scatter.8
  134.8 33.2 reduce-scatter.10
  171.2 28.0 reduce-scatter.12
  202.3 51.3 reduce-scatter.14
where the time goes:
time: 388 us; the launch traced here: 387 us
  waiting for transfers between devices  179 us (46%)
  blocking collectives  125 us (32%)
  starting transfers between devices  31.1 us (8%)
  local copies, waits for them, and re-layouts  23.3 us (6%)
  between operations  14 us (4%)
  matrix products  9.47 us (2%)
  other arithmetic  5.13 us (1%)
    reduce_scatter x2, waiting for transfers between devices, own_block(): parts = lax.psum_scatter(parts, axes[k], scatter_dimension=0, tiled=True)  88.6 us
    all_gather x4, blocking collectives, stacked_from(): parts = lax.all_gather(parts, axes[k], axis=0, tiled=True)  59.4 us
    all_gather x1, blocking collectives, per_device(): upstream = lax.all_gather(cotangent, 'fsdp', axis=0, tiled=True)  54.1 us
    unnamed x6, waiting for transfers between devices  53.7 us
    all_to_all x1, waiting for transfers between devices, sent_and_summed(): parts = lax.all_to_all(cut_along(shard, dim, peers), axis, 0, 0, tiled=True)  36.6 us
    all_to_all x1, starting transfers between devices, sent_and_summed(): parts = lax.all_to_all(cut_along(shard, dim, peers), axis, 0, 0, tiled=True)  24 us
    all_to_all x1, blocking collectives, per_device(): lax.all_to_all(new_weight, 'tensor', split_axis=0, concat_axis=1, tiled=T...  12 us
  transfers between devices with their start and end apart: 6, of which 5 were waited for; matrix products, arithmetic and copies ran while one was open for 4% of the time, Pallas kernels for 0%

commit v1 on v0

v1 whole, which is shorter than its diff:
```python
import jax
import jax.numpy as jnp
from jax import lax
from jax.experimental import pallas as pl
from jax.experimental.pallas import tpu as pltpu
from jax.sharding import Mesh
from jax.sharding import PartitionSpec as P

HEAD_DIM = 128
GROUP_HEADS = 8
KV_HEADS = 4
STEPS = 4
ADAM_STEP = 10
GZ, GX, YH, YL, CO = "gz", "gx", "yh", "yl", "co"
GROUP = (GZ, GX)
FSDP = (YH, CO)
ALL = (GZ, GX, YH, CO, YL)
NX, NZ = 4, 12
QROWS = 512
PART = 48
STARTS = tuple(min(PART * k, QROWS - PART) for k in range(NZ))

learn_rate = 0.001
beta_one = 0.9
beta_two = 0.95
epsilon = 1e-08
decay_rate = 0.1
masked_score = -1e30


def apply_adamw(gradient, weight, moment_one, moment_two):
    first_new = beta_one * moment_one + (1.0 - beta_one) * gradient
    second_new = beta_two * moment_two + (1.0 - beta_two) * gradient * gradient
    first_hat = first_new / (1.0 - beta_one**ADAM_STEP)
    second_hat = second_new / (1.0 - beta_two**ADAM_STEP)
    stepped = weight.astype(jnp.float32) * (
        1.0 - learn_rate * decay_rate
    ) - learn_rate * first_hat / (jnp.sqrt(second_hat) + epsilon)
    return (stepped.astype(jnp.bfloat16), first_new, second_new)


def vmem(*shape_map):
    return pl.BlockSpec(memory_space=pltpu.VMEM)


def hbm():
    return pl.BlockSpec(memory_space=pl.ANY)


def pack_kernel(place, tokens, out, sems):
    other = 1 - place[0]
    copies = []
    for k in range(2):
        first = pl.multiple_of(k * 4096 + other * 2048, 2048)
        copies.append(
            pltpu.make_async_copy(
                tokens.at[:, pl.ds(first, 2048)], out.at[:, pl.ds(k * 2048, 2048)], sems.at[k]
            )
        )
    for c in copies:
        c.start()
    for c in copies:
        c.wait()


def pack_tokens(place, tokens):
    return pl.pallas_call(
        pack_kernel,
        out_shape=jax.ShapeDtypeStruct((128, 4096), jnp.bfloat16),
        in_specs=[pl.BlockSpec(memory_space=pltpu.SMEM), hbm()],
        out_specs=hbm(),
        scratch_shapes=[pltpu.SemaphoreType.DMA((2,))],
        name="pack_tokens",
    )(place, tokens)


def grad_kernel(place, own, recv, cot_own, cot_recv, out):
    t = place[1]
    cot = jnp.concatenate([cot_own[...], cot_recv[...]], axis=0)
    for k in range(NX):
        first = pl.multiple_of(((k + t) % NX) * QROWS, QROWS)
        tok = jnp.concatenate([own[:, pl.ds(first, QROWS)], recv[:, pl.ds(first, QROWS)]], axis=0)
        out[k, 0] = lax.dot_general(
            tok, cot, (((0,), (0,)), ((), ())), preferred_element_type=jnp.float32
        ).astype(jnp.bfloat16)


def partial_gradient(place, tokens, recv, cot_own, cot_recv):
    return pl.pallas_call(
        grad_kernel,
        out_shape=jax.ShapeDtypeStruct((NX, 2, QROWS, 128), jnp.bfloat16),
        grid_spec=pltpu.PrefetchScalarGridSpec(
            num_scalar_prefetch=1,
            grid=(2,),
            in_specs=[
                pl.BlockSpec((128, 2048), lambda i, p: (0, 2 * i + p[0])),
                pl.BlockSpec((128, 2048), lambda i, p: (0, i)),
                pl.BlockSpec((128, 128), lambda i, p: (0, 0)),
                pl.BlockSpec((128, 128), lambda i, p: (0, 0)),
            ],
            out_specs=pl.BlockSpec((NX, 1, QROWS, 128), lambda i, p: (0, i, 0, 0)),
        ),
        name="partial_gradient",
    )(place, tokens, recv, cot_own, cot_recv)


def sum_x_kernel(parts, out):
    for h in range(2):
        total = parts[0, h].astype(jnp.float32)
        for k in range(1, NX):
            total = total + parts[k, h].astype(jnp.float32)
        total = total.astype(jnp.bfloat16)
        for z in range(NZ):
            out[z, h] = total[STARTS[z] : STARTS[z] + PART]


def sum_over_x(parts):
    return pl.pallas_call(
        sum_x_kernel,
        out_shape=jax.ShapeDtypeStruct((NZ, 2, PART, 128), jnp.bfloat16),
        in_specs=[vmem()],
        out_specs=vmem(),
        name="sum_over_x",
    )(parts)


def shard_kernel(parts, weight, one, two, grad_out, weight_out):
    total = parts[0, 0].astype(jnp.float32)
    for z in range(NZ):
        for h in range(2):
            if z or h:
                total = total + parts[z, h].astype(jnp.float32)
    grad_out[...] = jnp.broadcast_to(total.astype(jnp.bfloat16)[None], grad_out.shape)
    weight_out[...] = apply_adamw(total, weight[...], one[...], two[...])[0]


def update_shard(parts, weight, one, two):
    return pl.pallas_call(
        shard_kernel,
        out_shape=(
            jax.ShapeDtypeStruct((NZ, PART, 128), jnp.bfloat16),
            jax.ShapeDtypeStruct((PART, 128), jnp.bfloat16),
        ),
        in_specs=[vmem()] * 4,
        out_specs=(vmem(), vmem()),
        name="update_shard",
    )(parts, weight, one, two)


def whole_quarter(parts):
    last = STARTS[NZ - 1]
    kept = [parts[k] for k in range(10)] + [parts[10][480 - last :]]
    return jnp.concatenate(kept, axis=0)


def join_kernel(parts, out):
    kept = [parts[k] for k in range(10)] + [parts[NZ - 2][480 - STARTS[NZ - 2] :]]
    whole = jnp.concatenate(kept, axis=0)
    for k in range(NX):
        out[k] = whole


def join_quarter(parts, name):
    return pl.pallas_call(
        join_kernel,
        out_shape=jax.ShapeDtypeStruct((NX, QROWS, 128), jnp.bfloat16),
        in_specs=[vmem()],
        out_specs=vmem(),
        name=name,
    )(parts)


def adamw_kernel(place, grad, weight, one, two, weight_out, one_out, two_out):
    new_weight, first, second = apply_adamw(
        grad[0].astype(jnp.float32), weight[...], one[...], two[...]
    )
    weight_out[...] = new_weight
    one_out[...] = first
    two_out[...] = second


def update_all(place, grad, weight, one, two):
    spot = lambda k, p: ((k + p[1]) % NX, 0)
    block = pl.BlockSpec((QROWS, 128), spot)
    shape = lambda d: jax.ShapeDtypeStruct((2048, 128), d)
    return pl.pallas_call(
        adamw_kernel,
        out_shape=(shape(jnp.bfloat16), shape(jnp.float32), shape(jnp.float32)),
        grid_spec=pltpu.PrefetchScalarGridSpec(
            num_scalar_prefetch=1,
            grid=(NX,),
            in_specs=[pl.BlockSpec((1, QROWS, 128), lambda k, p: (k, 0, 0)), block, block, block],
            out_specs=(block, block, block),
        ),
        name="update_all",
    )(place, grad, weight, one, two)


def joined_weight(place, parts, whole):
    t = place[1]
    for k in range(NX):
        first = pl.multiple_of(((t - k + NX) % NX) * 128, 128)
        whole[:, pl.ds(first, 128)] = parts[k]


def rows_times_weight(hidden, core, whole, out, extra):
    for s in range(STEPS):
        for h in range(2):
            value = jnp.dot(hidden[s, h, core], whole[...], preferred_element_type=jnp.float32)
            for l in range(4):
                piece = value[l * 16 : (l + 1) * 16]
                spot = h * 4 + l
                if extra is not None:
                    piece = piece + extra[spot, s * 16 : (s + 1) * 16].astype(jnp.float32)
                out[spot, s * 16 : (s + 1) * 16] = piece.astype(jnp.bfloat16)


def send_kernel(place, hidden, parts, out, whole):
    joined_weight(place, parts, whole)
    rows_times_weight(hidden, 1 - place[0], whole, out, None)


def keep_kernel(place, hidden, parts, recv, out, whole):
    joined_weight(place, parts, whole)
    rows_times_weight(hidden, place[0], whole, out, recv)


def values_part(place, hidden, parts, recv=None):
    args = (place, hidden, parts) + (() if recv is None else (recv,))
    return pl.pallas_call(
        send_kernel if recv is None else keep_kernel,
        out_shape=jax.ShapeDtypeStruct((8, STEPS * 16, 512), jnp.bfloat16),
        in_specs=[pl.BlockSpec(memory_space=pltpu.SMEM)] + [vmem()] * (len(args) - 1),
        out_specs=vmem(),
        scratch_shapes=[pltpu.VMEM((512, 512), jnp.bfloat16)],
        name="values_send" if recv is None else "values_keep",
    )(*args)


def attend_cached(queries, new_keys, key_cache, value_cache, lengths):
    row_total = lengths.shape[0]
    cache_len = key_cache.shape[1]
    query_b = queries.reshape(STEPS, row_total, KV_HEADS, GROUP_HEADS, HEAD_DIM)
    cached_keys = key_cache.reshape(row_total, cache_len, KV_HEADS, HEAD_DIM)
    cached_values = value_cache.reshape(row_total, cache_len, KV_HEADS, HEAD_DIM)
    fresh_keys = new_keys.reshape(STEPS, row_total, KV_HEADS, HEAD_DIM)
    score_scale = HEAD_DIM ** (-0.5)
    cached_scores = (
        jnp.einsum("tnhjd,nphd->nhjtp", query_b, cached_keys, preferred_element_type=jnp.float32)
        * score_scale
    )
    fresh_scores = (
        jnp.einsum("tnhjd,snhd->nhjts", query_b, fresh_keys, preferred_element_type=jnp.float32)
        * score_scale
    )
    cached_valid = jnp.arange(cache_len, dtype=jnp.int32)[None, :] < lengths[:, None]
    fresh_valid = (
        jnp.arange(STEPS, dtype=jnp.int32)[None, :] <= jnp.arange(STEPS, dtype=jnp.int32)[:, None]
    )
    cached_scores = jnp.where(cached_valid[:, None, None, None, :], cached_scores, masked_score)
    fresh_scores = jnp.where(fresh_valid[None, None, None, :, :], fresh_scores, masked_score)
    highest = jnp.maximum(jnp.max(cached_scores, axis=-1), jnp.max(fresh_scores, axis=-1))[
        ..., None
    ]
    cached_exp = jnp.exp(cached_scores - highest)
    fresh_exp = jnp.exp(fresh_scores - highest)
    denominator = jnp.sum(cached_exp, axis=-1, keepdims=True) + jnp.sum(
        fresh_exp, axis=-1, keepdims=True
    )
    cached_probs = (cached_exp / denominator).astype(jnp.bfloat16)
    fresh_probs = (fresh_exp / denominator).astype(jnp.bfloat16)
    result = jnp.einsum(
        "nhjtp,nphd->tnhjd", cached_probs, cached_values, preferred_element_type=jnp.float32
    )
    return result, fresh_probs


def attend_fresh(result, fresh_probs, fresh_values):
    row_total = result.shape[1]
    fresh_vals = fresh_values.reshape(STEPS, row_total, KV_HEADS, HEAD_DIM)
    result = result + jnp.einsum(
        "nhjts,snhd->tnhjd", fresh_probs, fresh_vals, preferred_element_type=jnp.float32
    )
    return result.reshape(STEPS, row_total, -1).astype(jnp.bfloat16)


def per_device(
    tokens,
    cotangent,
    weight,
    moment_one,
    moment_two,
    hidden,
    queries,
    new_keys,
    key_cache,
    value_cache,
    lengths,
):
    core, t = lax.axis_index(CO), lax.axis_index(YL)
    x, z = lax.axis_index(GX), lax.axis_index(GZ)
    place = jnp.stack([core, t]).astype(jnp.int32)
    swap = [(0, 1), (1, 0)]

    recv = lax.ppermute(pack_tokens(place, tokens), CO, swap)
    cot_recv = lax.ppermute(cotangent, CO, swap)
    parts = partial_gradient(place, tokens, recv, cotangent, cot_recv)
    parts = lax.all_to_all(parts, GX, 0, 0, tiled=True)
    parts = sum_over_x(parts).reshape(NZ * 2, PART, 128)
    parts = lax.all_to_all(parts, (GZ, YH), 0, 0, tiled=True).reshape(NZ, 2, PART, 128)

    first = ((x + t) % NX) * QROWS + jnp.minimum(PART * z, QROWS - PART)
    own = lambda a: lax.dynamic_slice_in_dim(a, first, PART, 0)
    grad_parts, shard = update_shard(parts, own(weight), own(moment_one), own(moment_two))

    turn = [(a * 4 + b, a * 4 + (a + b) % 4) for a in range(NX) for b in range(4)]
    shard = lax.ppermute(shard, (GX, YL), turn)
    weight_parts = lax.all_to_all(
        jnp.broadcast_to(shard[None], (NZ, PART, 128)), GZ, 0, 0, tiled=True
    )
    weight_parts = lax.all_to_all(join_quarter(weight_parts, "join_weight"), GX, 0, 0, tiled=True)

    hidden = hidden.reshape(STEPS, 2, 2, 64, 512)
    recv = lax.ppermute(values_part(place, hidden, weight_parts), CO, swap)
    values = values_part(place, hidden, weight_parts, recv)
    values = lax.all_to_all(values, (YH, YL), 0, 0, tiled=True)

    grad_parts = lax.all_to_all(grad_parts, GZ, 0, 0, tiled=True)
    grad_parts = lax.all_to_all(join_quarter(grad_parts, "join_grad"), GX, 0, 0, tiled=True)
    new_weight, first_new, second_new = update_all(
        place, grad_parts, weight, moment_one, moment_two
    )

    result, fresh_probs = attend_cached(queries, new_keys, key_cache, value_cache, lengths)
    fresh = jnp.sum(values.astype(jnp.float32), axis=0).astype(jnp.bfloat16)
    attention = attend_fresh(result, fresh_probs, fresh.reshape(STEPS, 16, 512))
    return (new_weight, first_new, second_new, attention)


def solution(mesh):
    split = Mesh(mesh.devices.reshape(NZ, NX, 2, 2, 4), (GZ, GX, YH, CO, YL))
    rows, cols = FSDP, YL
    return jax.shard_map(
        per_device,
        mesh=split,
        in_specs=(
            P(GROUP + FSDP, None),
            P(GROUP + FSDP, cols),
            P(rows, cols),
            P(rows, cols),
            P(rows, cols),
            P(None, GROUP, FSDP + (YL,)),
            P(None, ALL, None),
            P(None, ALL, None),
            P(ALL, None, None),
            P(ALL, None, None),
            P(ALL),
        ),
        out_specs=(P(rows, cols), P(rows, cols), P(rows, cols), P(None, ALL, None)),
        check_vma=False,
    )
```

time: 388 us -> 196 us (0.51)
  the two profiles are of different devices: /device:TPU:9 before, /device:TPU:2 now
where the time goes in v1:
time: 196 us; the launch traced here: 195 us
  Pallas kernels  55.9 us (29%)
  blocking collectives  54.3 us (28%)
  waiting for transfers between devices  33.6 us (17%)
  starting transfers between devices  32.8 us (17%)
  local copies, waits for them, and re-layouts  9.6 us (5%)
  matrix products  5.61 us (3%)
  other arithmetic  2.09 us (1%)
    pallas_call x1, Pallas kernels, pack_tokens(): pl.pallas_call(pack_kernel, out_shape=jax.ShapeDtypeStruct((128, 4096), j...  33.5 us
    all_to_all x1, blocking collectives, per_device(): parts = lax.all_to_all(parts, GX, 0, 0, tiled=True)  28.3 us
    all_to_all x1, waiting for transfers between devices, per_device(): lax.all_to_all(parts, (GZ, YH), 0, 0, tiled=True).reshape(NZ, 2, PART, 128)  17.4 us
    all_to_all x1, blocking collectives, per_device(): lax.all_to_all(jnp.broadcast_to(shard[None], (NZ, PART, 128)), GZ, 0, 0,...  16 us
    all_to_all x1, starting transfers between devices, per_device(): lax.all_to_all(parts, (GZ, YH), 0, 0, tiled=True).reshape(NZ, 2, PART, 128)  11.6 us
    all_to_all x1, blocking collectives, per_device(): lax.all_to_all(join_quarter(weight_parts, 'join_weight'), GX, 0, 0, tiled...  10 us
    all_to_all x1, waiting for transfers between devices, per_device(): grad_parts = lax.all_to_all(grad_parts, GZ, 0, 0, tiled=True)  7.1 us
    pallas_call x2, Pallas kernels, values_part(): pl.pallas_call(send_kernel if recv is None else keep_kernel, out_shape=ja...  6.41 us
  transfers between devices with their start and end apart: 8, of which 6 were waited for; matrix products, arithmetic and copies ran while one was open for 5% of the time, Pallas kernels for 7%

profile of v1, /device:TPU:2, one launch (start us, length us, event | category | flops | bytes accessed | tf_op | source)
XLA Modules:
  0.0 194.7 jit_solution(5963329275711663593)
XLA Ops:
  1.3 33.5 %pack_tokens.1 = bf16[128,4096]{1,0:T(8,128)(2,1)} custom-call(s32[2]{0:T(128)} %pad_add_fusion.place, bf16[128,8192]{1,0:T(8,128)(2,1)} %own.1), custom_call_target="tpu_custom_call" | custom-call | tf_op jit(solution)/shard_map/pack_tokens/pallas_call | solution.py:67
  34.8 1.9 collective-permute-start
  36.8 2.4 %collective-permute-start.1 = (bf16[128,128]{1,0:T(8,128)(2,1)S(1)}, bf16[128,128]{1,0:T(8,128)(2,1)S(1)}, u32[]{:S(2)}, u32[]{:S(2)}) collective-permute-start(bf16[128,128]{1,0:T(8,128)(2,1)S(1)} %copy-done.10), channel_id=1, source_target_pairs={{0,4},{4,0},{1,5},{5,1},{2,6},{6,2},{3,7},{7,3},{8,12},{12,8},{9,1... | collective-permute-start | bytes 98312 | tf_op jit(solution)/shard_map/ppermute | solution.py:306
  40.6 1.0 copy-done.2
  41.6 3.7 %partial_gradient.1 = bf16[4,2,512,128]{3,2,1,0:T(8,128)(2,1)} custom-call(s32[2]{0:T(128)} %pad_add_fusion.place, bf16[128,8192]{1,0:T(8,128)(2,1)} %own.1, bf16[128,4096]{1,0:T(8,128)(2,1)} %copy-done.2, bf16[128,128]{1,0:T(8,128)(2,1)} %cot_own.1, bf16[128,128]{1,0:T(8,128)(2,1)} %copy-done.11), custom_call_target="tpu_custom_call" | custom-call | tf_op jit(solution)/shard_map/partial_gradient/pallas_call | solution.py:89
  45.3 28.3 %all_to_all.35.parts = bf16[4,2,512,128]{3,2,1,0:T(8,128)(2,1)} all-to-all(bf16[4,2,512,128]{3,2,1,0:T(8,128)(2,1)} %partial_gradient.1), channel_id=1, replica_groups=mesh['gz'=12,'gx'=4,'yh'=2,'co'=2,'yl'=4] {'gx'}, dimensions={0} | all-to-all | bytes 2097152 | tf_op jit(solution)/shard_map/all_to_all | solution.py:308
  73.6 2.1 %sum_over_x.1 = bf16[12,2,48,128]{3,2,1,0:T(8,128)(2,1)} custom-call(bf16[4,2,512,128]{3,2,1,0:T(8,128)(2,1)} %all_to_all.35.parts), custom_call_target="tpu_custom_call" | custom-call | tf_op jit(solution)/shard_map/sum_over_x/pallas_call | solution.py:118
  75.7 11.6 %all-to-all-start.1 = ((bf16[24,48,128]{2,1,0:T(8,128)(2,1)}), bf16[24,48,128]{2,1,0:T(8,128)(2,1)S(1)}, u32[]{:S(2)}, u32[]{:S(2)}) async-start(bf16[24,48,128]{2,1,0:T(8,128)(2,1)} %bitcast.32), calls=%async_computation.1 | async-start | bytes 589824 | tf_op jit(solution)/shard_map/all_to_all | solution.py:310
  87.3 1.3 constant_dynamic-slice_fusion.2.weight
  88.7 1.4 constant_dynamic-slice_fusion
  90.1 17.4 %all-to-all-done.1 = bf16[24,48,128]{2,1,0:T(8,128)(2,1)S(1)} async-done(((bf16[24,48,128]{2,1,0:T(8,128)(2,1)}), bf16[24,48,128]{2,1,0:T(8,128)(2,1)S(1)}, u32[]{:S(2)}, u32[]{:S(2)}) %all-to-all-start.1) | async-done | bytes 294944 | tf_op jit(solution)/shard_map/all_to_all | solution.py:310
  108.2 1.7 update_shard.1
  109.9 2.6 %collective-permute-start.2 = (bf16[48,128]{1,0:T(8,128)(2,1)}, bf16[48,128]{1,0:T(8,128)(2,1)S(1)}, u32[]{:S(2)}, u32[]{:S(2)}) collective-permute-start(bf16[48,128]{1,0:T(8,128)(2,1)} %get-tuple-element.13), channel_id=1, source_target_pairs={{0,0},{1,1},{2,2},{3,3},{16,17},{17,18},{18,19},{19,16},{32,34},{3... | collective-permute-start | bytes 36872 | tf_op jit(solution)/shard_map/ppermute | solution.py:317
  112.5 5.0 %collective-permute-done.2 = bf16[48,128]{1,0:T(8,128)(2,1)S(1)} collective-permute-done((bf16[48,128]{1,0:T(8,128)(2,1)}, bf16[48,128]{1,0:T(8,128)(2,1)S(1)}, u32[]{:S(2)}, u32[]{:S(2)}) %collective-permute-start.2) | collective-permute-done | bytes 12320 | tf_op jit(solution)/shard_map/ppermute | solution.py:317
  117.5 16.0 %all_to_all.36.parts = bf16[12,48,128]{2,1,0:T(8,128)(2,1)} all-to-all(bf16[12,48,128]{2,1,0:T(8,128)(2,1)S(1)} %broadcast_in_dim.43), channel_id=1, replica_groups=mesh['gz'=12,'gx'=4,'yh'=2,'co'=2,'yl'=4] {'gz'}, dimensions={0} | all-to-all | bytes 294912 | tf_op jit(solution)/shard_map/all_to_all | solution.py:318
  133.5 1.8 join_weight.1
  135.3 10.0 %all_to_all.37.parts = bf16[4,512,128]{2,1,0:T(8,128)(2,1)} all-to-all(bf16[4,512,128]{2,1,0:T(8,128)(2,1)} %join_weight.1), channel_id=1, replica_groups=mesh['gz'=12,'gx'=4,'yh'=2,'co'=2,'yl'=4] {'gx'}, dimensions={0} | all-to-all | bytes 1048576 | tf_op jit(solution)/shard_map/all_to_all | solution.py:321
  145.3 3.7 %all-to-all-start.2 = ((bf16[12,48,128]{2,1,0:T(8,128)(2,1)}), bf16[12,48,128]{2,1,0:T(8,128)(2,1)S(1)}, u32[]{:S(2)}, u32[]{:S(2)}) async-start(bf16[12,48,128]{2,1,0:T(8,128)(2,1)} %get-tuple-element.9), calls=%async_computation.2 | async-start | bytes 294912 | tf_op jit(solution)/shard_map/all_to_all | solution.py:328
  149.0 3.2 %values_send.1 = bf16[8,64,512]{2,1,0:T(8,128)(2,1)} custom-call(s32[2]{0:T(128)} %pad_add_fusion.place, bf16[4,2,2,64,512]{4,3,2,1,0:T(8,128)(2,1)} %bitcast.29, bf16[4,512,128]{2,1,0:T(8,128)(2,1)} %all_to_all.37.parts), custom_call_target="tpu_custom_call" | custom-call | tf_op jit(solution)/shard_map/values_send/pallas_call | solution.py:230
  152.1 2.0 %collective-permute-start.3 = (bf16[8,64,512]{2,1,0:T(8,128)(2,1)}, bf16[8,64,512]{2,1,0:T(8,128)(2,1)S(1)}, u32[]{:S(2)}, u32[]{:S(2)}) collective-permute-start(bf16[8,64,512]{2,1,0:T(8,128)(2,1)} %values_send.1), channel_id=1, source_target_pairs={{0,4},{4,0},{1,5},{5,1},{2,6},{6,2},{3,7},{7,3},{8,12},{12,8},{9,1... | collective-permute-start | bytes 1572872 | tf_op jit(solution)/shard_map/ppermute | solution.py:324
  154.2 7.1 %all-to-all-done.2.parts = bf16[12,48,128]{2,1,0:T(8,128)(2,1)S(1)} async-done(((bf16[12,48,128]{2,1,0:T(8,128)(2,1)}), bf16[12,48,128]{2,1,0:T(8,128)(2,1)S(1)}, u32[]{:S(2)}, u32[]{:S(2)}) %all-to-all-start.2) | async-done | bytes 147488 | tf_op jit(solution)/shard_map/all_to_all | solution.py:328
  161.9 1.8 join_grad.1
  163.7 5.0 %all-to-all-start.3 = ((bf16[4,512,128]{2,1,0:T(8,128)(2,1)}), bf16[4,512,128]{2,1,0:T(8,128)(2,1)S(1)}, u32[]{:S(2)}, u32[]{:S(2)}) async-start(bf16[4,512,128]{2,1,0:T(8,128)(2,1)} %join_grad.1), calls=%async_computation.3 | async-start | bytes 1048576 | tf_op jit(solution)/shard_map/all_to_all | solution.py:329
  169.6 0.9 reshape.74
  171.6 3.3 %values_keep.1 = bf16[8,64,512]{2,1,0:T(8,128)(2,1)} custom-call(s32[2]{0:T(128)} %pad_add_fusion.place, bf16[4,2,2,64,512]{4,3,2,1,0:T(8,128)(2,1)} %bitcast.30, bf16[4,512,128]{2,1,0:T(8,128)(2,1)} %all_to_all.37.parts, bf16[8,64,512]{2,1,0:T(8,128)(2,1)} %copy-done.8), custom_call_target="tpu_custom_call" | custom-call | tf_op jit(solution)/shard_map/values_keep/pallas_call | solution.py:230
  175.4 3.5 %all-to-all-start.6 = ((bf16[8,64,512]{2,1,0:T(8,128)(2,1)}), bf16[8,64,512]{2,1,0:T(8,128)(2,1)S(1)}, u32[]{:S(2)}, u32[]{:S(2)}) async-start(bf16[8,64,512]{2,1,0:T(8,128)(2,1)} %values_keep.1), calls=%async_computation.6 | async-start | bytes 1048576 | tf_op jit(solution)/shard_map/all_to_all | solution.py:326
  178.9 2.5 %fusion.19 = (f32[16,4,8,4]{2,3,1,0:T(4,128)S(1)}, f32[16,4,8,4,4]{2,4,3,1,0:T(4,128)S(1)}) fusion(bf16[4,16,4,8,128]{4,3,2,1,0:T(8,128)(2,1)S(1)} %bitcast.36, bf16[4,16,4,128,1]{3,2,1,0,4:T(4,128)(2,1)S(1)} %bitcast.38, pred[4,4]{1,0:T(4,128)(4,1)S(1)} %iota_compare_fusion.1), kind=kOutput, calls=%fused_computation.33 | convolution fusion | flops 2119680 | bytes 630800 | tf_op jit(solution)/shard_map/tnhjd,snhd->nhjts/dot_general | solution.py:253
  181.3 1.7 fusion.18
  184.4 5.0 %update_all.1 = (bf16[2048,128]{1,0:T(8,128)(2,1)}, f32[2048,128]{1,0:T(8,128)}, f32[2048,128]{1,0:T(8,128)}) custom-call(s32[2]{0:T(128)} %pad_add_fusion.place, bf16[4,512,128]{2,1,0:T(8,128)(2,1)} %copy-done, bf16[2048,128]{1,0:T(8,128)(2,1)} %weight.1, f32[2048,128]{1,0:T(8,128)} %one.1, f32[2048,128]{1,0:T(8,128)} %two.1), custom_call_target="tpu_custom_call" | custom-call | tf_op jit(solution)/shard_map/update_all/pallas_call | solution.py:186
  189.4 2.7 %all-to-all-done.6 = bf16[8,64,512]{2,1,0:T(8,128)(2,1)S(1)} async-done(((bf16[8,64,512]{2,1,0:T(8,128)(2,1)}), bf16[8,64,512]{2,1,0:T(8,128)(2,1)S(1)}, u32[]{:S(2)}, u32[]{:S(2)}) %all-to-all-start.6) | async-done | bytes 524320 | tf_op jit(solution)/shard_map/all_to_all | solution.py:326
  192.7 1.0 fusion.3
  193.7 1.0 convert_element_type.17
  (44 shorter events, 7.9 us)
Async XLA Ops:
  0.6 36.1 %copy-start.10 = (bf16[128,128]{1,0:T(8,128)(2,1)S(1)}, bf16[128,128]{1,0:T(8,128)(2,1)}, u32[]{:S(2)}) copy-start(bf16[128,128]{1,0:T(8,128)(2,1)} %cot_own.1) | copy-start | bytes 98308
  34.8 5.2 %collective-permute-start = (bf16[128,4096]{1,0:T(8,128)(2,1)}, bf16[128,4096]{1,0:T(8,128)(2,1)S(1)}, u32[]{:S(2)}, u32[]{:S(2)}) collective-permute-start(bf16[128,4096]{1,0:T(8,128)(2,1)} %pack_tokens.1), channel_id=1, source_target_pairs={{0,4},{4,0},{1,5},{5,1},{2,6},{6,2},{3,7},{7,3},{8,12},{12,8},{9,1... | collective-permute-start | bytes 3145736 | tf_op jit(solution)/shard_map/ppermute | solution.py:305
  36.8 3.3 %collective-permute-start.1 = (bf16[128,128]{1,0:T(8,128)(2,1)S(1)}, bf16[128,128]{1,0:T(8,128)(2,1)S(1)}, u32[]{:S(2)}, u32[]{:S(2)}) collective-permute-start(bf16[128,128]{1,0:T(8,128)(2,1)S(1)} %copy-done.10), channel_id=1, source_target_pairs={{0,4},{4,0},{1,5},{5,1},{2,6},{6,2},{3,7},{7,3},{8,12},{12,8},{9,1... | collective-permute-start | bytes 98312 | tf_op jit(solution)/shard_map/ppermute | solution.py:306
  40.0 0.6 copy-start.11
  40.6 1.0 copy-start.2
  75.7 31.8 %all-to-all-start.1 = ((bf16[24,48,128]{2,1,0:T(8,128)(2,1)}), bf16[24,48,128]{2,1,0:T(8,128)(2,1)S(1)}, u32[]{:S(2)}, u32[]{:S(2)}) async-start(bf16[24,48,128]{2,1,0:T(8,128)(2,1)} %bitcast.32), calls=%async_computation.1 | async-start | bytes 589824 | tf_op jit(solution)/shard_map/all_to_all | solution.py:310
  107.5 0.7 copy-start.1
  109.9 7.6 %collective-permute-start.2 = (bf16[48,128]{1,0:T(8,128)(2,1)}, bf16[48,128]{1,0:T(8,128)(2,1)S(1)}, u32[]{:S(2)}, u32[]{:S(2)}) collective-permute-start(bf16[48,128]{1,0:T(8,128)(2,1)} %get-tuple-element.13), channel_id=1, source_target_pairs={{0,0},{1,1},{2,2},{3,3},{16,17},{17,18},{18,19},{19,16},{32,34},{3... | collective-permute-start | bytes 36872 | tf_op jit(solution)/shard_map/ppermute | solution.py:317
  145.3 23.5 %copy-start.4 = (bf16[4,16,4096]{2,1,0:T(8,128)(2,1)S(1)}, bf16[4,16,4096]{2,1,0:T(8,128)(2,1)}, u32[]{:S(2)}) copy-start(bf16[4,16,4096]{2,1,0:T(8,128)(2,1)} %param.17) | copy-start | bytes 1572868
  145.3 16.0 %all-to-all-start.2 = ((bf16[12,48,128]{2,1,0:T(8,128)(2,1)}), bf16[12,48,128]{2,1,0:T(8,128)(2,1)S(1)}, u32[]{:S(2)}, u32[]{:S(2)}) async-start(bf16[12,48,128]{2,1,0:T(8,128)(2,1)} %get-tuple-element.9), calls=%async_computation.2 | async-start | bytes 294912 | tf_op jit(solution)/shard_map/all_to_all | solution.py:328
  149.0 20.7 %copy-start.5 = (bf16[16,32,512]{2,1,0:T(8,128)(2,1)S(1)}, bf16[16,32,512]{2,1,0:T(8,128)(2,1)}, u32[]{:S(2)}) copy-start(bf16[16,32,512]{2,1,0:T(8,128)(2,1)} %param.19) | copy-start | bytes 1572868
  152.1 18.4 %copy-start.9 = (bf16[4,16,512]{2,1,0:T(8,128)(2,1)S(1)}, bf16[4,16,512]{2,1,0:T(8,128)(2,1)}, u32[]{:S(2)}) copy-start(bf16[4,16,512]{2,1,0:T(8,128)(2,1)} %param.18) | copy-start | bytes 196612
  152.1 18.5 %copy-start.6 = (bf16[16,32,512]{2,1,0:T(8,128)(2,1)S(1)}, bf16[16,32,512]{2,1,0:T(8,128)(2,1)}, u32[]{:S(2)}) copy-start(bf16[16,32,512]{2,1,0:T(8,128)(2,1)} %param.20) | copy-start | bytes 1572868
  152.1 18.7 %collective-permute-start.3 = (bf16[8,64,512]{2,1,0:T(8,128)(2,1)}, bf16[8,64,512]{2,1,0:T(8,128)(2,1)S(1)}, u32[]{:S(2)}, u32[]{:S(2)}) collective-permute-start(bf16[8,64,512]{2,1,0:T(8,128)(2,1)} %values_send.1), channel_id=1, source_target_pairs={{0,4},{4,0},{1,5},{5,1},{2,6},{6,2},{3,7},{7,3},{8,12},{12,8},{9,1... | collective-permute-start | bytes 1572872 | tf_op jit(solution)/shard_map/ppermute | solution.py:324
  161.3 0.7 copy-start.3
  163.7 7.0 %copy-start.12 = (s32[16]{0:T(128)S(1)}, s32[16]{0:T(128)}, u32[]{:S(2)}) copy-start(s32[16]{0:T(128)} %param.21) | copy-start | bytes 196
  163.7 11.7 %all-to-all-start.3 = ((bf16[4,512,128]{2,1,0:T(8,128)(2,1)}), bf16[4,512,128]{2,1,0:T(8,128)(2,1)S(1)}, u32[]{:S(2)}, u32[]{:S(2)}) async-start(bf16[4,512,128]{2,1,0:T(8,128)(2,1)} %join_grad.1), calls=%async_computation.3 | async-start | bytes 1048576 | tf_op jit(solution)/shard_map/all_to_all | solution.py:329
  170.7 8.1 %copy-start.7 = (bf16[8,8,32,128]{3,2,1,0:T(8,128)(2,1)S(1)}, bf16[8,8,32,128]{3,2,1,0:T(8,128)(2,1)}, u32[]{:S(2)}) copy-start(bf16[8,8,32,128]{3,2,1,0:T(8,128)(2,1)} %copy.39) | copy-start | bytes 1572868
  170.8 0.8 copy-start.8
  175.4 7.7 %copy-start = (bf16[4,512,128]{2,1,0:T(8,128)(2,1)}, bf16[4,512,128]{2,1,0:T(8,128)(2,1)S(1)}, u32[]{:S(2)}) copy-start(bf16[4,512,128]{2,1,0:T(8,128)(2,1)S(1)} %all-to-all-done.3.grad) | copy-start | bytes 1572868
  175.4 16.7 %all-to-all-start.6 = ((bf16[8,64,512]{2,1,0:T(8,128)(2,1)}), bf16[8,64,512]{2,1,0:T(8,128)(2,1)S(1)}, u32[]{:S(2)}, u32[]{:S(2)}) async-start(bf16[8,64,512]{2,1,0:T(8,128)(2,1)} %values_keep.1), calls=%async_computation.6 | async-start | bytes 1048576 | tf_op jit(solution)/shard_map/all_to_all | solution.py:326

commit v2 on v1

v2 whole, which is shorter than its diff:
```python
import jax
import jax.numpy as jnp
from jax import lax
from jax.experimental import pallas as pl
from jax.experimental.pallas import tpu as pltpu
from jax.sharding import Mesh
from jax.sharding import PartitionSpec as P

HEAD_DIM = 128
GROUP_HEADS = 8
KV_HEADS = 4
STEPS = 4
ADAM_STEP = 10
GZ, GX, YH, YL, CO = "gz", "gx", "yh", "yl", "co"
GROUP = (GZ, GX)
FSDP = (YH, CO)
ALL = (GZ, GX, YH, CO, YL)
NX, NZ = 4, 12
QROWS = 512
PART = 48
STARTS = tuple(min(PART * k, QROWS - PART) for k in range(NZ))

learn_rate = 0.001
beta_one = 0.9
beta_two = 0.95
epsilon = 1e-08
decay_rate = 0.1
masked_score = -1e30


def apply_adamw(gradient, weight, moment_one, moment_two):
    first_new = beta_one * moment_one + (1.0 - beta_one) * gradient
    second_new = beta_two * moment_two + (1.0 - beta_two) * gradient * gradient
    first_hat = first_new / (1.0 - beta_one**ADAM_STEP)
    second_hat = second_new / (1.0 - beta_two**ADAM_STEP)
    stepped = weight.astype(jnp.float32) * (
        1.0 - learn_rate * decay_rate
    ) - learn_rate * first_hat / (jnp.sqrt(second_hat) + epsilon)
    return (stepped.astype(jnp.bfloat16), first_new, second_new)


def vmem():
    return pl.BlockSpec(memory_space=pltpu.VMEM)


def wide(t):
    return t[0] // 2


def pack_kernel(t, tokens, out):
    out[...] = tokens[...]


def pack_tokens(t, tokens):
    return pl.pallas_call(
        pack_kernel,
        out_shape=jax.ShapeDtypeStruct((128, 4096), jnp.bfloat16),
        grid_spec=pltpu.PrefetchScalarGridSpec(
            num_scalar_prefetch=1,
            grid=(4,),
            in_specs=[pl.BlockSpec((128, 1024), lambda i, t: (0, 2 * i + wide(t)))],
            out_specs=pl.BlockSpec((128, 1024), lambda i, t: (0, i)),
        ),
        name="pack_tokens",
    )(t, tokens)


def grad_kernel(t, core, own_0, own_1, recv, cot_0, cot_1, out):
    b = t[0] % 2
    cot = jnp.concatenate([cot_0[...], cot_1[...]], axis=0)
    for rows, own in enumerate((own_0, own_1)):
        tok = jnp.concatenate([own[...], recv[:, rows * 1024 : (rows + 1) * 1024]], axis=0)
        value = lax.dot_general(
            tok, cot, (((0,), (0,)), ((), ())), preferred_element_type=jnp.float32
        ).astype(jnp.bfloat16)
        first = 2 * (core[0] ^ rows)
        out[first + b, 0] = value[:QROWS]
        out[first + (1 - b), 0] = value[QROWS:]


def partial_gradient(t, core, tokens, recv, cot_0, cot_1):
    return pl.pallas_call(
        grad_kernel,
        out_shape=jax.ShapeDtypeStruct((NX, 2, QROWS, 128), jnp.bfloat16),
        grid_spec=pltpu.PrefetchScalarGridSpec(
            num_scalar_prefetch=2,
            grid=(2,),
            in_specs=[
                pl.BlockSpec((128, 1024), lambda i, t, c: (0, 4 * i + wide(t))),
                pl.BlockSpec((128, 1024), lambda i, t, c: (0, 4 * i + 2 + wide(t))),
                pl.BlockSpec((128, 2048), lambda i, t, c: (0, i)),
                pl.BlockSpec((128, 128), lambda i, t, c: (0, 0)),
                pl.BlockSpec((128, 128), lambda i, t, c: (0, 0)),
            ],
            out_specs=pl.BlockSpec((NX, 1, QROWS, 128), lambda i, t, c: (0, i, 0, 0)),
        ),
        name="partial_gradient",
    )(t, core, tokens, tokens, recv, cot_0, cot_1)


def sum_x_kernel(parts, out):
    for h in range(2):
        total = parts[0, h].astype(jnp.float32)
        for k in range(1, NX):
            total = total + parts[k, h].astype(jnp.float32)
        total = total.astype(jnp.bfloat16)
        for z in range(NZ):
            out[z, h] = total[STARTS[z] : STARTS[z] + PART]


def sum_over_x(parts):
    return pl.pallas_call(
        sum_x_kernel,
        out_shape=jax.ShapeDtypeStruct((NZ, 2, PART, 128), jnp.bfloat16),
        in_specs=[vmem()],
        out_specs=vmem(),
        name="sum_over_x",
    )(parts)


def shard_kernel(parts, out):
    total = parts[0].astype(jnp.float32)
    for k in range(1, NZ * 2):
        total = total + parts[k].astype(jnp.float32)
    total = total.astype(jnp.bfloat16)
    for k in range(NZ * NX):
        out[k] = total


def sum_over_z(parts):
    return pl.pallas_call(
        shard_kernel,
        out_shape=jax.ShapeDtypeStruct((NZ * NX, PART, 128), jnp.bfloat16),
        in_specs=[vmem()],
        out_specs=vmem(),
        name="sum_over_z",
    )(parts)


def whole_block(parts, k):
    last = 480 - STARTS[NZ - 2]
    kept = [parts[z, k] for z in range(10)] + [parts[NZ - 2, k, last:]]
    return jnp.concatenate(kept, axis=0).astype(jnp.float32)


def adamw_kernel(t, core, back_0, back_1, weight, one, two, weight_out, one_out, two_out):
    for j, grad in enumerate((back_0, back_1)):

        @pl.when(pl.program_id(0) // 2 == j)
        def _():
            new_weight, first, second = apply_adamw(
                whole_block(grad, 0), weight[...], one[...], two[...]
            )
            weight_out[...] = new_weight
            one_out[...] = first
            two_out[...] = second


def update_all(t, core, back_0, back_1, weight, one, two):
    block = pl.BlockSpec(
        (QROWS, 128), lambda k, t, c: (t[0] ^ (2 * (c[0] ^ (k // 2))) ^ (k % 2), 0)
    )
    back = pl.BlockSpec((NZ, 1, PART, 128), lambda k, t, c: (0, k % 2, 0, 0))
    shape = lambda d: jax.ShapeDtypeStruct((2048, 128), d)
    return pl.pallas_call(
        adamw_kernel,
        out_shape=(shape(jnp.bfloat16), shape(jnp.float32), shape(jnp.float32)),
        grid_spec=pltpu.PrefetchScalarGridSpec(
            num_scalar_prefetch=2,
            grid=(NX,),
            in_specs=[back, back, block, block, block],
            out_specs=(block, block, block),
        ),
        name="update_all",
    )(t, core, back_0, back_1, weight, one, two)


def values_kernel(t, parts, state_0, state_1, own, near, far_own, far_near, out, whole):
    b = t[0] % 2

    @pl.when(pl.program_id(0) == 0)
    def _():
        for j, state in enumerate((state_0, state_1)):
            for i in range(2):
                rows = pl.ds(pl.multiple_of((b ^ i) * QROWS, QROWS), QROWS)
                p = 2 * j + i
                whole[p * QROWS : (p + 1) * QROWS] = apply_adamw(
                    whole_block(parts, p),
                    state[0, rows],
                    state[1, rows].astype(jnp.float32),
                    state[2, rows].astype(jnp.float32),
                )[0]

    value = None
    for p, rows in enumerate((own, near, far_own, far_near)):
        part = jnp.dot(
            rows[0], whole[p * QROWS : (p + 1) * QROWS], preferred_element_type=jnp.float32
        )
        value = part if value is None else value + part
    value = value.astype(jnp.bfloat16)
    for d in range(16):
        out[d] = value[d * 16 : (d + 1) * 16]


def values_part(t, parts, state_0, state_1, own, near, far_own, far_near):
    rows = pl.BlockSpec((1, 256, 512), lambda s, t: (s, 0, 0))
    state = pl.BlockSpec((3, 1024, 128), lambda s, t: (0, 0, 0))
    return pl.pallas_call(
        values_kernel,
        out_shape=jax.ShapeDtypeStruct((16, STEPS * 16, 128), jnp.bfloat16),
        grid_spec=pltpu.PrefetchScalarGridSpec(
            num_scalar_prefetch=1,
            grid=(STEPS,),
            in_specs=[
                pl.BlockSpec((NZ, NX, PART, 128), lambda s, t: (0, 0, 0, 0)),
                state,
                state,
                rows,
                rows,
                rows,
                rows,
            ],
            out_specs=pl.BlockSpec((16, 16, 128), lambda s, t: (0, s, 0)),
            scratch_shapes=[pltpu.VMEM((4 * QROWS, 128), jnp.bfloat16)],
        ),
        name="values_part",
    )(t, parts, state_0, state_1, own, near, far_own, far_near)


def attend_cached(queries, new_keys, key_cache, value_cache, lengths):
    row_total = lengths.shape[0]
    cache_len = key_cache.shape[1]
    query_b = queries.reshape(STEPS, row_total, KV_HEADS, GROUP_HEADS, HEAD_DIM)
    cached_keys = key_cache.reshape(row_total, cache_len, KV_HEADS, HEAD_DIM)
    cached_values = value_cache.reshape(row_total, cache_len, KV_HEADS, HEAD_DIM)
    fresh_keys = new_keys.reshape(STEPS, row_total, KV_HEADS, HEAD_DIM)
    score_scale = HEAD_DIM ** (-0.5)
    cached_scores = (
        jnp.einsum("tnhjd,nphd->nhjtp", query_b, cached_keys, preferred_element_type=jnp.float32)
        * score_scale
    )
    fresh_scores = (
        jnp.einsum("tnhjd,snhd->nhjts", query_b, fresh_keys, preferred_element_type=jnp.float32)
        * score_scale
    )
    cached_valid = jnp.arange(cache_len, dtype=jnp.int32)[None, :] < lengths[:, None]
    fresh_valid = (
        jnp.arange(STEPS, dtype=jnp.int32)[None, :] <= jnp.arange(STEPS, dtype=jnp.int32)[:, None]
    )
    cached_scores = jnp.where(cached_valid[:, None, None, None, :], cached_scores, masked_score)
    fresh_scores = jnp.where(fresh_valid[None, None, None, :, :], fresh_scores, masked_score)
    highest = jnp.maximum(jnp.max(cached_scores, axis=-1), jnp.max(fresh_scores, axis=-1))[
        ..., None
    ]
    cached_exp = jnp.exp(cached_scores - highest)
    fresh_exp = jnp.exp(fresh_scores - highest)
    denominator = jnp.sum(cached_exp, axis=-1, keepdims=True) + jnp.sum(
        fresh_exp, axis=-1, keepdims=True
    )
    cached_probs = (cached_exp / denominator).astype(jnp.bfloat16)
    fresh_probs = (fresh_exp / denominator).astype(jnp.bfloat16)
    result = jnp.einsum(
        "nhjtp,nphd->hjtnd", cached_probs, cached_values, preferred_element_type=jnp.float32
    ).reshape(KV_HEADS, -1, HEAD_DIM)
    spread = jnp.transpose(fresh_probs, (1, 2, 3, 0, 4))[..., None]
    same = jnp.eye(row_total, dtype=jnp.bool_)[None, None, None, :, None, :]
    spread = jnp.where(same, spread, jnp.zeros((), jnp.bfloat16))
    return result, spread.reshape(KV_HEADS, -1, STEPS * row_total)


def finish_kernel(values, result, spread, out):
    for h in range(KV_HEADS):
        total = None
        for k in range(2):
            for c in range(2):
                for v in (h & 1, (h & 1) + 2):
                    if (v ^ (2 * c)) == h:
                        part = values[k * 8 + c * 4 + v].astype(jnp.float32)
                        total = part if total is None else total + part
        value = result[h] + jnp.dot(
            spread[h], total.astype(jnp.bfloat16), preferred_element_type=jnp.float32
        )
        value = value.astype(jnp.bfloat16)
        for j in range(GROUP_HEADS):
            first = (h * GROUP_HEADS + j) * HEAD_DIM
            out[:, first : first + HEAD_DIM] = value[j * 64 : (j + 1) * 64]


def finish_attention(values, result, spread):
    return pl.pallas_call(
        finish_kernel,
        out_shape=jax.ShapeDtypeStruct((64, 4096), jnp.bfloat16),
        in_specs=[vmem()] * 3,
        out_specs=vmem(),
        name="finish_attention",
    )(values, result, spread)


def per_device(
    tokens,
    cotangent,
    weight,
    moment_one,
    moment_two,
    hidden,
    queries,
    new_keys,
    key_cache,
    value_cache,
    lengths,
):
    c, y = lax.axis_index(CO), lax.axis_index(YL)
    core, t = c.astype(jnp.int32).reshape(1), y.astype(jnp.int32).reshape(1)
    swap = [(0, 1), (1, 0)]
    spots = [(k, v) for k in range(2) for v in range(4)]
    bring = [[((k ^ j) * 4 + (v ^ (2 * k)), k * 4 + v) for k, v in spots] for j in range(2)]
    back = [[(d, s) for s, d in pairs] for pairs in bring]

    cots = [lax.ppermute(cotangent, (CO, YL), pairs) for pairs in bring]
    packed = pack_tokens(t, tokens)
    recv = lax.ppermute(packed, CO, swap)
    parts = partial_gradient(t, core, tokens, recv, *cots)
    near = lax.ppermute(hidden, YL, [(0, 1), (1, 0), (2, 3), (3, 2)])
    queries, new_keys, key_cache, value_cache, parts = lax.optimization_barrier(
        (queries, new_keys, key_cache, value_cache, parts)
    )
    states = []
    for j in range(2):
        first = ((y // 2) ^ c ^ j) * 1024
        states.append(
            jnp.stack(
                [
                    lax.dynamic_slice_in_dim(v, first, 1024, 0).astype(jnp.bfloat16)
                    for v in (weight, moment_one, moment_two)
                ]
            )
        )
    parts = lax.all_to_all(parts, GX, 0, 0, tiled=True)
    parts = sum_over_x(parts).reshape(NZ * 2, PART, 128)
    hidden, near, _ = lax.optimization_barrier((hidden, near, parts))
    parts = lax.all_to_all(parts, (GZ, YH), 0, 0, tiled=True)

    far = lax.ppermute(hidden, CO, swap)
    far_near = lax.ppermute(near, CO, swap)
    states = [lax.ppermute(v, (CO, YL), pairs) for v, pairs in zip(states, bring)]
    result, spread = attend_cached(queries, new_keys, key_cache, value_cache, lengths)
    parts, result, spread = lax.optimization_barrier((parts, result, spread))

    parts = sum_over_z(parts)
    grads = lax.all_to_all(parts, GROUP, 0, 0, tiled=True)
    grads = grads.reshape(NZ, NX, PART, 128)
    owned = [
        lax.ppermute(grads[:, 2 * j : 2 * j + 2], (CO, YL), back[j]) for j in range(2)
    ]
    values = values_part(t, grads, *states, hidden, near, far, far_near)
    values = lax.all_to_all(values, (YH, CO, YL), 0, 0, tiled=True)
    new_weight, first_new, second_new = update_all(t, core, *owned, weight, moment_one, moment_two)

    attention = finish_attention(values, result, spread).reshape(STEPS, 16, 4096)
    return (new_weight, first_new, second_new, attention)


def solution(mesh):
    split = Mesh(mesh.devices.reshape(NZ, NX, 2, 2, 4), (GZ, GX, YH, CO, YL))
    rows, cols = FSDP, YL
    return jax.shard_map(
        per_device,
        mesh=split,
        in_specs=(
            P(GROUP + FSDP, None),
            P(GROUP + FSDP, cols),
            P(rows, cols),
            P(rows, cols),
            P(rows, cols),
            P(None, GROUP, FSDP + (YL,)),
            P(None, ALL, None),
            P(None, ALL, None),
            P(ALL, None, None),
            P(ALL, None, None),
            P(ALL),
        ),
        out_specs=(P(rows, cols), P(rows, cols), P(rows, cols), P(None, ALL, None)),
        check_vma=False,
    )
```

time: 196 us -> 178 us (0.908)
  blocking collectives: 54.3 us -> 0 us
  starting transfers between devices: 32.8 us -> 82.9 us
  Pallas kernels: 55.9 us -> 23.7 us
  local copies, waits for them, and re-layouts: 9.6 us -> 18.9 us
  waiting for transfers between devices: 33.6 us -> 42.5 us
    all_to_all x3 -> x0, blocking collectives: 54.3 us -> none  [the longest x1 28.3 us: per_device(): parts = lax.all_to_all(parts, GX, 0, 0, tiled=True)]
    pallas_call x1, Pallas kernels: 33.5 us -> 3.38 us  [pack_tokens(): pl.pallas_call(pack_kernel, out_shape=jax.ShapeDtypeStruct((128, 4096), j...]
    all_to_all x4, starting transfers between devices: 23.8 us -> 53 us  [the longest x1 21.2 us: per_device(): values = lax.all_to_all(values, (YH, CO, YL), 0, 0, tiled=True)]
    ppermute x4 -> x10, waiting for transfers between devices: 5.86 us -> 29.8 us  [the longest x2 15.2 us: per_device(): lax.ppermute(v, (CO, YL), pairs)]
    ppermute x4 -> x10, starting transfers between devices: 8.93 us -> 29.9 us  [the longest x2 7.17 us: per_device(): lax.ppermute(v, (CO, YL), pairs)]
    all_to_all x4, waiting for transfers between devices: 27.7 us -> 12.7 us  [the longest x1 6.37 us: per_device(): parts = lax.all_to_all(parts, (GZ, YH), 0, 0, tiled=True)]
    broadcast_in_dim x1 -> x6, local copies, waits for them, and re-layouts: 0.02 us -> 6.17 us  [attend_cached(): spread = jnp.where(same, spread, jnp.zeros((), jnp.bfloat16))]
    transpose x0 -> x1, local copies, waits for them, and re-layouts: none -> 2.83 us  [attend_cached(): jnp.einsum('nhjtp,nphd->hjtnd', cached_probs, cached_values, preferred_el...]
  transfers between devices with their start and end apart: 8 -> 14, of which waited for: 6 -> 4; matrix products, arithmetic and copies ran while one was open for 5% -> 12% of each run, Pallas kernels for 7% -> 7%
where the time goes in v2:
time: 178 us; the launch traced here: 177 us
  starting transfers between devices  82.9 us (47%)
  waiting for transfers between devices  42.5 us (24%)
  Pallas kernels  23.7 us (13%)
  local copies, waits for them, and re-layouts  18.9 us (11%)
  matrix products  5.71 us (3%)
  other arithmetic  2.32 us (1%)
    all_to_all x1, starting transfers between devices, per_device(): values = lax.all_to_all(values, (YH, CO, YL), 0, 0, tiled=True)  21.2 us
    ppermute x2, waiting for transfers between devices, per_device(): lax.ppermute(v, (CO, YL), pairs)  15.2 us
    ppermute x2, waiting for transfers between devices, per_device(): lax.ppermute(grads[:, 2 * j:2 * j + 2], (CO, YL), back[j])  14.6 us
    all_to_all x1, starting transfers between devices, per_device(): parts = lax.all_to_all(parts, (GZ, YH), 0, 0, tiled=True)  13 us
    all_to_all x1, starting transfers between devices, per_device(): parts = lax.all_to_all(parts, GX, 0, 0, tiled=True)  11.6 us
    all_to_all x1, starting transfers between devices, per_device(): grads = lax.all_to_all(parts, GROUP, 0, 0, tiled=True)  7.2 us
    ppermute x2, starting transfers between devices, per_device(): lax.ppermute(v, (CO, YL), pairs)  7.17 us
    unnamed x47, local copies, waits for them, and re-layouts  6.58 us
  transfers between devices with their start and end apart: 14, of which 4 were waited for; matrix products, arithmetic and copies ran while one was open for 12% of the time, Pallas kernels for 7%

profile of v2, /device:TPU:2, one launch (start us, length us, event | category | flops | bytes accessed | tf_op | source)
XLA Modules:
  0.0 177.2 jit_solution(8125877195285258994)
XLA Ops:
  0.7 3.4 %pack_tokens.1 = bf16[128,4096]{1,0:T(8,128)(2,1)} custom-call(s32[1]{0:T(128)} %bitcast.t, bf16[128,8192]{1,0:T(8,128)(2,1)} %own_1.1), custom_call_target="tpu_custom_call" | custom-call | tf_op jit(solution)/shard_map/pack_tokens/pallas_call | solution.py:55
  4.0 1.9 %collective-permute-start = (bf16[128,4096]{1,0:T(8,128)(2,1)}, bf16[128,4096]{1,0:T(8,128)(2,1)S(1)}, u32[]{:S(2)}, u32[]{:S(2)}) collective-permute-start(bf16[128,4096]{1,0:T(8,128)(2,1)} %pack_tokens.1), channel_id=1, source_target_pairs={{0,4},{4,0},{1,5},{5,1},{2,6},{6,2},{3,7},{7,3},{8,12},{12,8},{9,1... | collective-permute-start | bytes 3145736 | tf_op jit(solution)/shard_map/ppermute | solution.py:321
  6.6 5.9 %collective-permute-start.2 = (bf16[128,128]{1,0:T(8,128)(2,1)S(1)}, bf16[128,128]{1,0:T(8,128)(2,1)S(1)}, u32[]{:S(2)}, u32[]{:S(2)}) collective-permute-start(bf16[128,128]{1,0:T(8,128)(2,1)S(1)} %copy-done.22), channel_id=1, source_target_pairs={{4,0},{5,1},{6,2},{7,3},{2,4},{3,5},{0,6},{1,7},{12,8},{13,9},{14,... | collective-permute-start | bytes 98312 | tf_op jit(solution)/shard_map/ppermute | solution.py:319
  12.5 3.5 %collective-permute-start.7 = (bf16[4,256,512]{2,1,0:T(8,128)(2,1)}, bf16[4,256,512]{2,1,0:T(8,128)(2,1)}, u32[]{:S(2)}, u32[]{:S(2)}) collective-permute-start(bf16[4,256,512]{2,1,0:T(8,128)(2,1)} %own), channel_id=1, source_target_pairs={{0,1},{1,0},{2,3},{3,2},{4,5},{5,4},{6,7},{7,6},{8,9},{9,8},{10,11... | collective-permute-start | bytes 3145736 | tf_op jit(solution)/shard_map/ppermute | solution.py:323
  18.8 3.1 %partial_gradient.1 = bf16[4,2,512,128]{3,2,1,0:T(8,128)(2,1)} custom-call(s32[1]{0:T(128)} %bitcast.t, s32[1]{0:T(128)} %bitcast.1.core, bf16[128,8192]{1,0:T(8,128)(2,1)} %own_1.1, bf16[128,8192]{1,0:T(8,128)(2,1)} %own_1.1, bf16[128,4096]{1,0:T(8,128)(2,1)} %copy-done.8, bf16[128,128]{1,0:T(8,128)(2,1)} %copy-done.19, bf16[128,128]{1,0:T(8,128)(2,1)} %copy-done.20), custom_call_target="tpu_custom_call" | custom-call | tf_op jit(solution)/shard_map/partial_gradient/pallas_call | solution.py:82
  22.1 11.6 %all-to-all-start = ((bf16[4,2,512,128]{3,2,1,0:T(8,128)(2,1)}), bf16[4,2,512,128]{3,2,1,0:T(8,128)(2,1)S(1)}, u32[]{:S(2)}, u32[]{:S(2)}) async-start(bf16[4,2,512,128]{3,2,1,0:T(8,128)(2,1)} %partial_gradient.1), calls=%async_computation | async-start | bytes 2097152 | tf_op jit(solution)/shard_map/all_to_all | solution.py:338
  33.7 2.4 %fusion.6 = f32[16,4,4,4,8]{4,2,3,1,0:T(4,128)S(1)} fusion(bf16[4,16,4,8,128]{4,3,2,1,0:T(8,128)(2,1)S(1)} %bitcast.55, bf16[4,16,4,128,1]{3,2,1,0,4:T(4,128)(2,1)S(1)} %bitcast.63), kind=kOutput, calls=%fused_computation.17 | convolution fusion | flops 2097152 | bytes 622592 | tf_op jit(solution)/shard_map/tnhjd,snhd->nhjts/dot_general | solution.py:243
  38.8 0.9 reshape.92
  39.7 6.3 %all-to-all-done.parts = bf16[4,2,512,128]{3,2,1,0:T(8,128)(2,1)S(1)} async-done(((bf16[4,2,512,128]{3,2,1,0:T(8,128)(2,1)}), bf16[4,2,512,128]{3,2,1,0:T(8,128)(2,1)S(1)}, u32[]{:S(2)}, u32[]{:S(2)}) %all-to-all-start) | async-done | bytes 1048608 | tf_op jit(solution)/shard_map/all_to_all | solution.py:338
  46.0 1.0 copy-done.1
  47.0 2.1 %sum_over_x.1 = bf16[12,2,48,128]{3,2,1,0:T(8,128)(2,1)} custom-call(bf16[4,2,512,128]{3,2,1,0:T(8,128)(2,1)} %copy-done.1), custom_call_target="tpu_custom_call" | custom-call | tf_op jit(solution)/shard_map/sum_over_x/pallas_call | solution.py:112
  49.0 13.0 %all-to-all-start.1 = ((bf16[24,48,128]{2,1,0:T(8,128)(2,1)}), bf16[24,48,128]{2,1,0:T(8,128)(2,1)S(1)}, u32[]{:S(2)}, u32[]{:S(2)}) async-start(bf16[24,48,128]{2,1,0:T(8,128)(2,1)} %bitcast.57), calls=%async_computation.1 | async-start | bytes 589824 | tf_op jit(solution)/shard_map/all_to_all | solution.py:341
  62.1 2.8 %convolution_bitcast_fusion = f32[4,8,4,16,128]{4,1,2,3,0:T(8,128)} fusion(bf16[16,32,4,128,1]{3,2,1,0,4:T(4,128)(2,1)} %bitcast.60, f32[16,4,8,4,32]{4,2,3,1,0:T(8,128)S(1)} %get-tuple-element.39, f32[16,4,8,4]{2,3,1,0:T(4,128)S(1)} %add.23, f32[16,4,8,4]{2,3,1,0:T(4,128)S(1)} %max.11), kind=kOutput, calls=%fused_computation | convolution fusion | flops 16973824 | bytes 1851392 | tf_op jit(solution)/shard_map/nhjtp,nphd->hjtnd/dot_general | solution.py:262
  65.7 3.6 %broadcast_in_dim.75 = bf16[4,512,64]{1,2,0:T(8,128)(2,1)S(1)} reshape(bf16[4,8,4,16,4,16]{3,2,1,5,4,0:T(4,128)(2,1)S(1)} %broadcast_in_dim.74) | data formatting | bytes 524288 | tf_op jit(solution)/shard_map/jit(_where)/broadcast_in_dim | solution.py:267
  69.6 2.8 %copy.70 = f32[4,8,4,16,128]{4,3,2,1,0:T(8,128)} copy(f32[4,8,4,16,128]{4,1,2,3,0:T(8,128)} %convolution_bitcast_fusion) | data formatting | bytes 2097152 | tf_op jit(solution)/shard_map/nhjtp,nphd->hjtnd/transpose | solution.py:262
  72.4 0.8 broadcast_select_fusion.spread
  73.3 6.4 %all-to-all-done.1.parts = bf16[24,48,128]{2,1,0:T(8,128)(2,1)S(1)} async-done(((bf16[24,48,128]{2,1,0:T(8,128)(2,1)}), bf16[24,48,128]{2,1,0:T(8,128)(2,1)S(1)}, u32[]{:S(2)}, u32[]{:S(2)}) %all-to-all-start.1) | async-done | bytes 294944 | tf_op jit(solution)/shard_map/all_to_all | solution.py:341
  80.3 1.9 %sum_over_z.1 = bf16[48,48,128]{2,1,0:T(8,128)(2,1)} custom-call(bf16[24,48,128]{2,1,0:T(8,128)(2,1)} %copy-done.5), custom_call_target="tpu_custom_call" | custom-call | tf_op jit(solution)/shard_map/sum_over_z/pallas_call | solution.py:131
  82.2 7.2 %all-to-all-start.2 = ((bf16[48,48,128]{2,1,0:T(8,128)(2,1)}), bf16[48,48,128]{2,1,0:T(8,128)(2,1)S(1)}, u32[]{:S(2)}, u32[]{:S(2)}) async-start(bf16[48,48,128]{2,1,0:T(8,128)(2,1)} %sum_over_z.1), calls=%async_computation.2 | async-start | bytes 1179648 | tf_op jit(solution)/shard_map/all_to_all | solution.py:350
  89.7 1.9 %collective-permute-start.8 = (bf16[4,256,512]{2,1,0:T(8,128)(2,1)}, bf16[4,256,512]{2,1,0:T(8,128)(2,1)S(1)}, u32[]{:S(2)}, u32[]{:S(2)}) collective-permute-start(bf16[4,256,512]{2,1,0:T(8,128)(2,1)} %own), channel_id=1, source_target_pairs={{0,4},{4,0},{1,5},{5,1},{2,6},{6,2},{3,7},{7,3},{8,12},{12,8},{9,1... | collective-permute-start | bytes 3145736 | tf_op jit(solution)/shard_map/ppermute | solution.py:343
  91.6 2.4 %collective-permute-start.9 = (bf16[4,256,512]{2,1,0:T(8,128)(2,1)}, bf16[4,256,512]{2,1,0:T(8,128)(2,1)S(1)}, u32[]{:S(2)}, u32[]{:S(2)}) collective-permute-start(bf16[4,256,512]{2,1,0:T(8,128)(2,1)} %collective-permute-done.7.near), channel_id=1, source_target_pairs={{0,4},{4,0},{1,5},{5,1},{2,6},{6,2},{3,7},{7,3},{8,12},{12,8},{9,1... | collective-permute-start | bytes 3145736 | tf_op jit(solution)/shard_map/ppermute | solution.py:344
  94.9 6.5 %collective-permute-start.6 = (bf16[3,1024,128]{2,1,0:T(8,128)(2,1)S(1)}, bf16[3,1024,128]{2,1,0:T(8,128)(2,1)S(1)}, u32[]{:S(2)}, u32[]{:S(2)}) collective-permute-start(bf16[3,1024,128]{2,1,0:T(8,128)(2,1)S(1)} %pad_maximum_fusion.1), channel_id=1, source_target_pairs={{4,0},{5,1},{6,2},{7,3},{2,4},{3,5},{0,6},{1,7},{12,8},{13,9},{14,... | collective-permute-start | bytes 2359304 | tf_op jit(solution)/shard_map/ppermute | solution.py:345
  101.4 15.2 %collective-permute-done.6.state_1 = bf16[3,1024,128]{2,1,0:T(8,128)(2,1)S(1)} collective-permute-done((bf16[3,1024,128]{2,1,0:T(8,128)(2,1)S(1)}, bf16[3,1024,128]{2,1,0:T(8,128)(2,1)S(1)}, u32[]{:S(2)}, u32[]{:S(2)}) %collective-permute-start.6) | collective-permute-done | bytes 786464 | tf_op jit(solution)/shard_map/ppermute | solution.py:345
  116.6 0.9 copy-done.11
  117.5 0.9 copy-done.7
  119.0 6.2 %values_part.1 = bf16[16,64,128]{2,1,0:T(8,128)(2,1)} custom-call(s32[1]{0:T(128)} %bitcast.t, bf16[12,4,48,128]{3,2,1,0:T(8,128)(2,1)} %bitcast.51, bf16[3,1024,128]{2,1,0:T(8,128)(2,1)} %copy-done.10, bf16[3,1024,128]{2,1,0:T(8,128)(2,1)} %copy-done.11, bf16[4,256,512]{2,1,0:T(8,128)(2,1)} %own, bf16[4,256,512]{2,1,0:T(8,128)(2,1)} %collective-permute-done.7.near, ...), custom_call_target="tpu_custom_call" | custom-call | tf_op jit(solution)/shard_map/values_part/pallas_call | solution.py:208
  125.2 21.2 %all-to-all-start.3 = ((bf16[16,64,128]{2,1,0:T(8,128)(2,1)}), bf16[16,64,128]{2,1,0:T(8,128)(2,1)S(1)}, u32[]{:S(2)}, u32[]{:S(2)}) async-start(bf16[16,64,128]{2,1,0:T(8,128)(2,1)} %values_part.1), calls=%async_computation.3 | async-start | bytes 524288 | tf_op jit(solution)/shard_map/all_to_all | solution.py:356
  146.4 1.1 fusion.19
  148.2 5.8 %collective-permute-start.4 = (bf16[12,2,48,128]{3,2,1,0:T(8,128)(2,1)S(1)}, bf16[12,2,48,128]{3,2,1,0:T(8,128)(2,1)S(1)}, u32[]{:S(2)}, u32[]{:S(2)}) collective-permute-start(bf16[12,2,48,128]{3,2,1,0:T(8,128)(2,1)S(1)} %get-tuple-element.34), channel_id=1, source_target_pairs={{0,4},{1,5},{2,6},{3,7},{4,2},{5,3},{6,0},{7,1},{8,12},{9,13},{10,... | collective-permute-start | bytes 884744 | tf_op jit(solution)/shard_map/ppermute | solution.py:353
  154.0 14.6 %collective-permute-done.4.back_1 = bf16[12,2,48,128]{3,2,1,0:T(8,128)(2,1)S(1)} collective-permute-done((bf16[12,2,48,128]{3,2,1,0:T(8,128)(2,1)S(1)}, bf16[12,2,48,128]{3,2,1,0:T(8,128)(2,1)S(1)}, u32[]{:S(2)}, u32[]{:S(2)}) %collective-permute-start.4) | collective-permute-done | bytes 294944 | tf_op jit(solution)/shard_map/ppermute | solution.py:353
  169.4 4.6 %update_all.1 = (bf16[2048,128]{1,0:T(8,128)(2,1)}, f32[2048,128]{1,0:T(8,128)}, f32[2048,128]{1,0:T(8,128)}) custom-call(s32[1]{0:T(128)} %bitcast.t, s32[1]{0:T(128)} %bitcast.1.core, bf16[12,2,48,128]{3,2,1,0:T(8,128)(2,1)} %copy-done.15, bf16[12,2,48,128]{3,2,1,0:T(8,128)(2,1)} %copy-done.16, bf16[2048,128]{1,0:T(8,128)(2,1)} %weight.1, ...), custom_call_target="tpu_custom_call" | custom-call | tf_op jit(solution)/shard_map/update_all/pallas_call | solution.py:165
  174.6 2.5 %finish_attention.1 = bf16[64,4096]{1,0:T(8,128)(2,1)} custom-call(bf16[16,64,128]{2,1,0:T(8,128)(2,1)} %copy-done.6, f32[4,512,128]{2,1,0:T(8,128)} %bitcast.53, bf16[4,512,64]{2,1,0:T(8,128)(2,1)} %broadcast_select_fusion.spread), custom_call_target="tpu_custom_call" | custom-call | tf_op jit(solution)/shard_map/finish_attention/pallas_call | solution.py:290
  (85 shorter events, 11.8 us)
Async XLA Ops:
  0.6 5.3 %copy-start.22 = (bf16[128,128]{1,0:T(8,128)(2,1)S(1)}, bf16[128,128]{1,0:T(8,128)(2,1)}, u32[]{:S(2)}) copy-start(bf16[128,128]{1,0:T(8,128)(2,1)} %param.12) | copy-start | bytes 98308
  0.6 15.4 %copy-start.21 = (s32[16]{0:T(128)S(1)}, s32[16]{0:T(128)}, u32[]{:S(2)}) copy-start(s32[16]{0:T(128)} %param.21) | copy-start | bytes 196
  4.0 13.8 %collective-permute-start = (bf16[128,4096]{1,0:T(8,128)(2,1)}, bf16[128,4096]{1,0:T(8,128)(2,1)S(1)}, u32[]{:S(2)}, u32[]{:S(2)}) collective-permute-start(bf16[128,4096]{1,0:T(8,128)(2,1)} %pack_tokens.1), channel_id=1, source_target_pairs={{0,4},{4,0},{1,5},{5,1},{2,6},{6,2},{3,7},{7,3},{8,12},{12,8},{9,1... | collective-permute-start | bytes 3145736 | tf_op jit(solution)/shard_map/ppermute | solution.py:321
  6.0 11.9 %collective-permute-start.1 = (bf16[128,128]{1,0:T(8,128)(2,1)S(1)}, bf16[128,128]{1,0:T(8,128)(2,1)S(1)}, u32[]{:S(2)}, u32[]{:S(2)}) collective-permute-start(bf16[128,128]{1,0:T(8,128)(2,1)S(1)} %copy-done.22), channel_id=1, source_target_pairs={{0,0},{1,1},{2,2},{3,3},{6,4},{7,5},{4,6},{5,7},{8,8},{9,9},{10,10... | collective-permute-start | bytes 98312 | tf_op jit(solution)/shard_map/ppermute | solution.py:319
  6.6 11.2 %collective-permute-start.2 = (bf16[128,128]{1,0:T(8,128)(2,1)S(1)}, bf16[128,128]{1,0:T(8,128)(2,1)S(1)}, u32[]{:S(2)}, u32[]{:S(2)}) collective-permute-start(bf16[128,128]{1,0:T(8,128)(2,1)S(1)} %copy-done.22), channel_id=1, source_target_pairs={{4,0},{5,1},{6,2},{7,3},{2,4},{3,5},{0,6},{1,7},{12,8},{13,9},{14,... | collective-permute-start | bytes 98312 | tf_op jit(solution)/shard_map/ppermute | solution.py:319
  12.5 77.1 %collective-permute-start.7 = (bf16[4,256,512]{2,1,0:T(8,128)(2,1)}, bf16[4,256,512]{2,1,0:T(8,128)(2,1)}, u32[]{:S(2)}, u32[]{:S(2)}) collective-permute-start(bf16[4,256,512]{2,1,0:T(8,128)(2,1)} %own), channel_id=1, source_target_pairs={{0,1},{1,0},{2,3},{3,2},{4,5},{5,4},{6,7},{7,6},{8,9},{9,8},{10,11... | collective-permute-start | bytes 3145736 | tf_op jit(solution)/shard_map/ppermute | solution.py:323
  17.9 1.0 copy-start.8
  18.8 3.1 %copy-start.12 = (bf16[4,16,4096]{2,1,0:T(8,128)(2,1)S(1)}, bf16[4,16,4096]{2,1,0:T(8,128)(2,1)}, u32[]{:S(2)}) copy-start(bf16[4,16,4096]{2,1,0:T(8,128)(2,1)} %param.17) | copy-start | bytes 1572868
  18.8 3.2 %copy-start.18 = (bf16[4,16,512]{2,1,0:T(8,128)(2,1)S(1)}, bf16[4,16,512]{2,1,0:T(8,128)(2,1)}, u32[]{:S(2)}) copy-start(bf16[4,16,512]{2,1,0:T(8,128)(2,1)} %param.18) | copy-start | bytes 196612
  22.1 14.5 %copy-start.13 = (bf16[16,32,512]{2,1,0:T(8,128)(2,1)S(1)}, bf16[16,32,512]{2,1,0:T(8,128)(2,1)}, u32[]{:S(2)}) copy-start(bf16[16,32,512]{2,1,0:T(8,128)(2,1)} %param.19) | copy-start | bytes 1572868
  22.1 23.9 %all-to-all-start = ((bf16[4,2,512,128]{3,2,1,0:T(8,128)(2,1)}), bf16[4,2,512,128]{3,2,1,0:T(8,128)(2,1)S(1)}, u32[]{:S(2)}, u32[]{:S(2)}) async-start(bf16[4,2,512,128]{3,2,1,0:T(8,128)(2,1)} %partial_gradient.1), calls=%async_computation | async-start | bytes 2097152 | tf_op jit(solution)/shard_map/all_to_all | solution.py:338
  37.3 1.5 copy-start.14
  46.0 1.0 copy-start.1
  49.0 30.6 %all-to-all-start.1 = ((bf16[24,48,128]{2,1,0:T(8,128)(2,1)}), bf16[24,48,128]{2,1,0:T(8,128)(2,1)S(1)}, u32[]{:S(2)}, u32[]{:S(2)}) async-start(bf16[24,48,128]{2,1,0:T(8,128)(2,1)} %bitcast.57), calls=%async_computation.1 | async-start | bytes 589824 | tf_op jit(solution)/shard_map/all_to_all | solution.py:341
  69.3 3.1 %copy-start.17 = (pred[512,64]{1,0:T(8,128)(4,1)S(1)}, pred[512,64]{1,0:T(8,128)(4,1)}, u32[]{:S(2)}) copy-start(pred[512,64]{1,0:T(8,128)(4,1)} %copy.71) | copy-start | bytes 98308
  72.4 17.0 %copy-start.4 = (bf16[2048,128]{1,0:T(8,128)(2,1)S(1)}, bf16[2048,128]{1,0:T(8,128)(2,1)}, u32[]{:S(2)}) copy-start(bf16[2048,128]{1,0:T(8,128)(2,1)} %weight.1) | copy-start | bytes 1572868
  72.4 17.1 %copy-start.2 = (f32[2048,128]{1,0:T(8,128)S(1)}, f32[2048,128]{1,0:T(8,128)}, u32[]{:S(2)}) copy-start(f32[2048,128]{1,0:T(8,128)} %one.1) | copy-start | bytes 3145732
  72.4 17.1 %copy-start.3 = (f32[2048,128]{1,0:T(8,128)S(1)}, f32[2048,128]{1,0:T(8,128)}, u32[]{:S(2)}) copy-start(f32[2048,128]{1,0:T(8,128)} %two.1) | copy-start | bytes 3145732
  82.2 35.3 %all-to-all-start.2 = ((bf16[48,48,128]{2,1,0:T(8,128)(2,1)}), bf16[48,48,128]{2,1,0:T(8,128)(2,1)S(1)}, u32[]{:S(2)}, u32[]{:S(2)}) async-start(bf16[48,48,128]{2,1,0:T(8,128)(2,1)} %sum_over_z.1), calls=%async_computation.2 | async-start | bytes 1179648 | tf_op jit(solution)/shard_map/all_to_all | solution.py:350
  89.7 26.9 %collective-permute-start.8 = (bf16[4,256,512]{2,1,0:T(8,128)(2,1)}, bf16[4,256,512]{2,1,0:T(8,128)(2,1)S(1)}, u32[]{:S(2)}, u32[]{:S(2)}) collective-permute-start(bf16[4,256,512]{2,1,0:T(8,128)(2,1)} %own), channel_id=1, source_target_pairs={{0,4},{4,0},{1,5},{5,1},{2,6},{6,2},{3,7},{7,3},{8,12},{12,8},{9,1... | collective-permute-start | bytes 3145736 | tf_op jit(solution)/shard_map/ppermute | solution.py:343
  91.6 25.9 %collective-permute-start.9 = (bf16[4,256,512]{2,1,0:T(8,128)(2,1)}, bf16[4,256,512]{2,1,0:T(8,128)(2,1)S(1)}, u32[]{:S(2)}, u32[]{:S(2)}) collective-permute-start(bf16[4,256,512]{2,1,0:T(8,128)(2,1)} %collective-permute-done.7.near), channel_id=1, source_target_pairs={{0,4},{4,0},{1,5},{5,1},{2,6},{6,2},{3,7},{7,3},{8,12},{12,8},{9,1... | collective-permute-start | bytes 3145736 | tf_op jit(solution)/shard_map/ppermute | solution.py:344
  94.1 7.3 %collective-permute-start.5 = (bf16[3,1024,128]{2,1,0:T(8,128)(2,1)S(1)}, bf16[3,1024,128]{2,1,0:T(8,128)(2,1)S(1)}, u32[]{:S(2)}, u32[]{:S(2)}) collective-permute-start(bf16[3,1024,128]{2,1,0:T(8,128)(2,1)S(1)} %pad_maximum_fusion), channel_id=1, source_target_pairs={{0,0},{1,1},{2,2},{3,3},{6,4},{7,5},{4,6},{5,7},{8,8},{9,9},{10,10... | collective-permute-start | bytes 2359304 | tf_op jit(solution)/shard_map/ppermute | solution.py:345
  94.9 21.6 %collective-permute-start.6 = (bf16[3,1024,128]{2,1,0:T(8,128)(2,1)S(1)}, bf16[3,1024,128]{2,1,0:T(8,128)(2,1)S(1)}, u32[]{:S(2)}, u32[]{:S(2)}) collective-permute-start(bf16[3,1024,128]{2,1,0:T(8,128)(2,1)S(1)} %pad_maximum_fusion.1), channel_id=1, source_target_pairs={{4,0},{5,1},{6,2},{7,3},{2,4},{3,5},{0,6},{1,7},{12,8},{13,9},{14,... | collective-permute-start | bytes 2359304 | tf_op jit(solution)/shard_map/ppermute | solution.py:345
  101.4 16.1 %copy-start.10 = (bf16[3,1024,128]{2,1,0:T(8,128)(2,1)}, bf16[3,1024,128]{2,1,0:T(8,128)(2,1)S(1)}, u32[]{:S(2)}) copy-start(bf16[3,1024,128]{2,1,0:T(8,128)(2,1)S(1)} %collective-permute-done.5.state_0) | copy-start | bytes 2359300
  116.6 0.9 copy-start.11
  117.5 1.0 copy-start.7
  117.5 1.3 copy-start.9
  117.5 1.5 copy-start
  125.2 48.7 %all-to-all-start.3 = ((bf16[16,64,128]{2,1,0:T(8,128)(2,1)}), bf16[16,64,128]{2,1,0:T(8,128)(2,1)S(1)}, u32[]{:S(2)}, u32[]{:S(2)}) async-start(bf16[16,64,128]{2,1,0:T(8,128)(2,1)} %values_part.1), calls=%async_computation.3 | async-start | bytes 524288 | tf_op jit(solution)/shard_map/all_to_all | solution.py:356
  147.5 6.5 %collective-permute-start.3 = (bf16[12,2,48,128]{3,2,1,0:T(8,128)(2,1)S(1)}, bf16[12,2,48,128]{3,2,1,0:T(8,128)(2,1)S(1)}, u32[]{:S(2)}, u32[]{:S(2)}) collective-permute-start(bf16[12,2,48,128]{3,2,1,0:T(8,128)(2,1)S(1)} %get-tuple-element.35), channel_id=1, source_target_pairs={{0,0},{1,1},{2,2},{3,3},{4,6},{5,7},{6,4},{7,5},{8,8},{9,9},{10,10... | collective-permute-start | bytes 884744 | tf_op jit(solution)/shard_map/ppermute | solution.py:353
  148.2 20.5 %collective-permute-start.4 = (bf16[12,2,48,128]{3,2,1,0:T(8,128)(2,1)S(1)}, bf16[12,2,48,128]{3,2,1,0:T(8,128)(2,1)S(1)}, u32[]{:S(2)}, u32[]{:S(2)}) collective-permute-start(bf16[12,2,48,128]{3,2,1,0:T(8,128)(2,1)S(1)} %get-tuple-element.34), channel_id=1, source_target_pairs={{0,4},{1,5},{2,6},{3,7},{4,2},{5,3},{6,0},{7,1},{8,12},{9,13},{10,... | collective-permute-start | bytes 884744 | tf_op jit(solution)/shard_map/ppermute | solution.py:353
  154.0 14.7 %copy-start.15 = (bf16[12,2,48,128]{3,2,1,0:T(8,128)(2,1)}, bf16[12,2,48,128]{3,2,1,0:T(8,128)(2,1)S(1)}, u32[]{:S(2)}) copy-start(bf16[12,2,48,128]{3,2,1,0:T(8,128)(2,1)S(1)} %collective-permute-done.3.back_0) | copy-start | bytes 884740
  (5 other events, 3.4 us)

commit v3 on v2

v3 whole, which is shorter than its diff:
```python
import jax
import jax.numpy as jnp
from jax import lax
from jax.experimental import pallas as pl
from jax.experimental.pallas import tpu as pltpu
from jax.sharding import Mesh
from jax.sharding import PartitionSpec as P

HEAD_DIM = 128
GROUP_HEADS = 8
KV_HEADS = 4
STEPS = 4
ADAM_STEP = 10
GZ, GX, YH, YL, CO = "gz", "gx", "yh", "yl", "co"
GROUP = (GZ, GX)
FSDP = (YH, CO)
ALL = (GZ, GX, YH, CO, YL)
NX, NZ = 4, 12
QROWS = 512
PART = 48
STARTS = tuple(min(PART * k, QROWS - PART) for k in range(NZ))

learn_rate = 0.001
beta_one = 0.9
beta_two = 0.95
epsilon = 1e-08
decay_rate = 0.1
masked_score = -1e30


def apply_adamw(gradient, weight, moment_one, moment_two):
    first_new = beta_one * moment_one + (1.0 - beta_one) * gradient
    second_new = beta_two * moment_two + (1.0 - beta_two) * gradient * gradient
    first_hat = first_new / (1.0 - beta_one**ADAM_STEP)
    second_hat = second_new / (1.0 - beta_two**ADAM_STEP)
    stepped = weight.astype(jnp.float32) * (
        1.0 - learn_rate * decay_rate
    ) - learn_rate * first_hat / (jnp.sqrt(second_hat) + epsilon)
    return (stepped.astype(jnp.bfloat16), first_new, second_new)


def vmem():
    return pl.BlockSpec(memory_space=pltpu.VMEM)


def wide(t):
    return t[0] // 2


def grad_kernel(t, core, own_0, own_1, recv_0, recv_1, cot_0, cot_1, out):
    b = t[0] % 2
    cot = jnp.concatenate([cot_0[...], cot_1[...]], axis=0)
    for rows, (own, recv) in enumerate(((own_0, recv_0), (own_1, recv_1))):
        tok = jnp.concatenate([own[...], recv[...]], axis=0)
        value = lax.dot_general(
            tok, cot, (((0,), (0,)), ((), ())), preferred_element_type=jnp.float32
        ).astype(jnp.bfloat16)
        first = 2 * (core[0] ^ rows)
        out[first + b, 0] = value[:QROWS]
        out[first + (1 - b), 0] = value[QROWS:]


def partial_gradient(t, core, tokens, recv, cot_0, cot_1):
    return pl.pallas_call(
        grad_kernel,
        out_shape=jax.ShapeDtypeStruct((NX, 2, QROWS, 128), jnp.bfloat16),
        grid_spec=pltpu.PrefetchScalarGridSpec(
            num_scalar_prefetch=2,
            grid=(2,),
            in_specs=[
                pl.BlockSpec((128, 1024), lambda i, t, c: (0, 4 * i + wide(t))),
                pl.BlockSpec((128, 1024), lambda i, t, c: (0, 4 * i + 2 + wide(t))),
                pl.BlockSpec((128, 1024), lambda i, t, c: (0, 4 * i + wide(t))),
                pl.BlockSpec((128, 1024), lambda i, t, c: (0, 4 * i + 2 + wide(t))),
                pl.BlockSpec((128, 128), lambda i, t, c: (0, 0)),
                pl.BlockSpec((128, 128), lambda i, t, c: (0, 0)),
            ],
            out_specs=pl.BlockSpec((NX, 1, QROWS, 128), lambda i, t, c: (0, i, 0, 0)),
        ),
        name="partial_gradient",
    )(t, core, tokens, tokens, recv, recv, cot_0, cot_1)


def sum_x_kernel(parts, out):
    for h in range(2):
        total = parts[0, h].astype(jnp.float32)
        for k in range(1, NX):
            total = total + parts[k, h].astype(jnp.float32)
        total = total.astype(jnp.bfloat16)
        for z in range(NZ):
            out[z, h] = total[STARTS[z] : STARTS[z] + PART]


def sum_over_x(parts):
    return pl.pallas_call(
        sum_x_kernel,
        out_shape=jax.ShapeDtypeStruct((NZ, 2, PART, 128), jnp.bfloat16),
        in_specs=[vmem()],
        out_specs=vmem(),
        name="sum_over_x",
    )(parts)


def shard_kernel(parts, state, grad_out, weight_out):
    total = parts[0].astype(jnp.float32)
    for k in range(1, NZ * 2):
        total = total + parts[k].astype(jnp.float32)
    grad_out[...] = total.astype(jnp.bfloat16)
    weight_out[...] = apply_adamw(total, state[0], state[1], state[2])[0]


def update_shard(parts, state):
    return pl.pallas_call(
        shard_kernel,
        out_shape=(jax.ShapeDtypeStruct((PART, 128), jnp.bfloat16),) * 2,
        in_specs=[vmem()] * 2,
        out_specs=(vmem(), vmem()),
        name="update_shard",
    )(parts, state)


def whole_block(parts, k):
    last = 480 - STARTS[NZ - 2]
    kept = [parts[z, k, 0] for z in range(10)] + [parts[NZ - 2, k, 0, last:]]
    return jnp.concatenate(kept, axis=0)


def adamw_kernel(t, core, grad, weight, one, two, weight_out, one_out, two_out):
    new_weight, first, second = apply_adamw(
        whole_block(grad, 0).astype(jnp.float32), weight[...], one[...], two[...]
    )
    weight_out[...] = new_weight
    one_out[...] = first
    two_out[...] = second


def update_all(t, core, both, weight, one, two):
    block = pl.BlockSpec(
        (QROWS, 128), lambda k, t, c: (t[0] ^ (2 * (c[0] ^ (k // 2))) ^ (k % 2), 0)
    )
    grad = pl.BlockSpec((NZ, 1, 1, PART, 128), lambda k, t, c: (0, k, 1, 0, 0))
    shape = lambda d: jax.ShapeDtypeStruct((2048, 128), d)
    return pl.pallas_call(
        adamw_kernel,
        out_shape=(shape(jnp.bfloat16), shape(jnp.float32), shape(jnp.float32)),
        grid_spec=pltpu.PrefetchScalarGridSpec(
            num_scalar_prefetch=2,
            grid=(NX,),
            in_specs=[grad, block, block, block],
            out_specs=(block, block, block),
        ),
        name="update_all",
    )(t, core, both, weight, one, two)


def values_kernel(parts, own, near, far_own, far_near, out, whole):
    @pl.when(pl.program_id(0) == 0)
    def _():
        for p in range(4):
            whole[p * QROWS : (p + 1) * QROWS] = whole_block(parts, p)

    value = None
    for p, rows in enumerate((own, near, far_own, far_near)):
        part = jnp.dot(
            rows[0], whole[p * QROWS : (p + 1) * QROWS], preferred_element_type=jnp.float32
        )
        value = part if value is None else value + part
    value = value.astype(jnp.bfloat16)
    for d in range(16):
        out[d] = value[d * 16 : (d + 1) * 16]


def values_part(both, own, near, far_own, far_near):
    rows = pl.BlockSpec((1, 256, 512), lambda s: (s, 0, 0))
    return pl.pallas_call(
        values_kernel,
        out_shape=jax.ShapeDtypeStruct((16, STEPS * 16, 128), jnp.bfloat16),
        grid=(STEPS,),
        in_specs=[
            pl.BlockSpec((NZ, NX, 1, PART, 128), lambda s: (0, 0, 0, 0, 0)),
            rows,
            rows,
            rows,
            rows,
        ],
        out_specs=pl.BlockSpec((16, 16, 128), lambda s: (0, s, 0)),
        scratch_shapes=[pltpu.VMEM((4 * QROWS, 128), jnp.bfloat16)],
        name="values_part",
    )(both, own, near, far_own, far_near)


def attend_cached(queries, new_keys, key_cache, lengths):
    row_total = lengths.shape[0]
    cache_len = key_cache.shape[1]
    query_b = queries.reshape(STEPS, row_total, KV_HEADS, GROUP_HEADS, HEAD_DIM)
    cached_keys = key_cache.reshape(row_total, cache_len, KV_HEADS, HEAD_DIM)
    fresh_keys = new_keys.reshape(STEPS, row_total, KV_HEADS, HEAD_DIM)
    score_scale = HEAD_DIM ** (-0.5)
    cached_scores = (
        jnp.einsum("tnhjd,nphd->nhjtp", query_b, cached_keys, preferred_element_type=jnp.float32)
        * score_scale
    )
    fresh_scores = (
        jnp.einsum("tnhjd,snhd->nhjts", query_b, fresh_keys, preferred_element_type=jnp.float32)
        * score_scale
    )
    cached_valid = jnp.arange(cache_len, dtype=jnp.int32)[None, :] < lengths[:, None]
    fresh_valid = (
        jnp.arange(STEPS, dtype=jnp.int32)[None, :] <= jnp.arange(STEPS, dtype=jnp.int32)[:, None]
    )
    cached_scores = jnp.where(cached_valid[:, None, None, None, :], cached_scores, masked_score)
    fresh_scores = jnp.where(fresh_valid[None, None, None, :, :], fresh_scores, masked_score)
    highest = jnp.maximum(jnp.max(cached_scores, axis=-1), jnp.max(fresh_scores, axis=-1))[
        ..., None
    ]
    cached_exp = jnp.exp(cached_scores - highest)
    fresh_exp = jnp.exp(fresh_scores - highest)
    denominator = jnp.sum(cached_exp, axis=-1, keepdims=True) + jnp.sum(
        fresh_exp, axis=-1, keepdims=True
    )
    cached_probs = (cached_exp / denominator).astype(jnp.bfloat16)
    fresh_probs = (fresh_exp / denominator).astype(jnp.bfloat16)
    return cached_probs, fresh_probs


def spread_probs(fresh_probs):
    row_total = fresh_probs.shape[0]
    spread = jnp.transpose(fresh_probs, (1, 2, 3, 0, 4))[..., None]
    same = jnp.eye(row_total, dtype=jnp.bool_)[None, None, None, :, None, :]
    spread = jnp.where(same, spread, jnp.zeros((), jnp.bfloat16))
    return spread.reshape(KV_HEADS, -1, STEPS * row_total)


def weigh_cached(cached_probs, value_cache):
    cached_values = value_cache.reshape(*value_cache.shape[:2], KV_HEADS, HEAD_DIM)
    return jnp.einsum(
        "nhjtp,nphd->hjtnd", cached_probs, cached_values, preferred_element_type=jnp.float32
    ).reshape(KV_HEADS, -1, HEAD_DIM)


def finish_kernel(first_0, first_1, second_0, second_1, result, spread, out):
    total = None
    for piece in (first_0, first_1, second_0, second_1):
        part = piece[0].astype(jnp.float32)
        total = part if total is None else total + part
    value = result[0] + jnp.dot(
        spread[0], total.astype(jnp.bfloat16), preferred_element_type=jnp.float32
    )
    value = value.astype(jnp.bfloat16)
    for j in range(GROUP_HEADS):
        out[:, j * HEAD_DIM : (j + 1) * HEAD_DIM] = value[j * 64 : (j + 1) * 64]


def finish_attention(values, result, spread):
    source = lambda k, c: pl.BlockSpec(
        (1, 64, 128), lambda h: (k * 8 + c * 4 + (h ^ (2 * c)), 0, 0)
    )
    return pl.pallas_call(
        finish_kernel,
        out_shape=jax.ShapeDtypeStruct((64, 4096), jnp.bfloat16),
        grid=(KV_HEADS,),
        in_specs=[
            source(0, 0),
            source(0, 1),
            source(1, 0),
            source(1, 1),
            pl.BlockSpec((1, 512, 128), lambda h: (h, 0, 0)),
            pl.BlockSpec((1, 512, 64), lambda h: (h, 0, 0)),
        ],
        out_specs=pl.BlockSpec((64, 1024), lambda h: (0, h)),
        name="finish_attention",
    )(values, values, values, values, result, spread)


def per_device(
    tokens,
    cotangent,
    weight,
    moment_one,
    moment_two,
    hidden,
    queries,
    new_keys,
    key_cache,
    value_cache,
    lengths,
):
    c, y = lax.axis_index(CO), lax.axis_index(YL)
    x, z = lax.axis_index(GX), lax.axis_index(GZ)
    core, t = c.astype(jnp.int32).reshape(1), y.astype(jnp.int32).reshape(1)
    swap = [(0, 1), (1, 0)]
    spots = [(k, v) for k in range(2) for v in range(4)]
    bring = [[((k ^ j) * 4 + (v ^ (2 * k)), k * 4 + v) for k, v in spots] for j in range(2)]

    cots = [lax.ppermute(cotangent, (CO, YL), pairs) for pairs in bring]
    recv = lax.ppermute(tokens, CO, swap)
    parts = partial_gradient(t, core, tokens, recv, *cots)
    queries, new_keys, key_cache, parts = lax.optimization_barrier(
        (queries, new_keys, key_cache, parts)
    )
    parts = lax.all_to_all(parts, GX, 0, 0, tiled=True)
    near = lax.ppermute(hidden, YL, [(0, 1), (1, 0), (2, 3), (3, 2)])

    j, i = x // 2, x % 2
    first = (y ^ (2 * (c ^ j)) ^ i) * QROWS + jnp.minimum(PART * z, QROWS - PART)
    state = jnp.stack(
        [
            lax.dynamic_slice_in_dim(v, first, PART, 0).astype(jnp.float32)
            for v in (weight, moment_one, moment_two)
        ]
    )
    turn = [(v * 8 + s, v * 8 + d) for v in range(NX) for s, d in bring[v // 2]]
    back = [(d, s) for s, d in turn]
    state = lax.ppermute(state, (GX, CO, YL), turn)

    parts = sum_over_x(parts).reshape(NZ * 2, PART, 128)
    parts = lax.all_to_all(parts, (GZ, YH), 0, 0, tiled=True)
    probs = attend_cached(queries, new_keys, key_cache, lengths)
    parts, state, probs = lax.optimization_barrier((parts, state, probs))
    grad, shard = update_shard(parts, state)

    grad = lax.ppermute(grad, (GX, CO, YL), back)
    both = jnp.broadcast_to(jnp.stack([shard, grad])[None], (NZ * NX, 2, PART, 128))
    both = lax.all_to_all(both, GROUP, 0, 0, tiled=True)
    both = both.reshape(NZ, NX, 2, PART, 128)
    far = lax.ppermute(hidden, CO, swap)
    far_near = lax.ppermute(near, CO, swap)
    cached_probs, fresh_probs = probs
    result = weigh_cached(cached_probs, value_cache)
    spread = spread_probs(fresh_probs)

    both, result, spread = lax.optimization_barrier((both, result, spread))
    values = values_part(both, hidden, near, far, far_near)
    values = lax.all_to_all(values, (YH, CO, YL), 0, 0, tiled=True)
    new_weight, first_new, second_new = update_all(t, core, both, weight, moment_one, moment_two)
    attention = finish_attention(values, result, spread).reshape(STEPS, 16, 4096)
    return (new_weight, first_new, second_new, attention)


def solution(mesh):
    split = Mesh(mesh.devices.reshape(NZ, NX, 2, 2, 4), (GZ, GX, YH, CO, YL))
    rows, cols = FSDP, YL
    return jax.shard_map(
        per_device,
        mesh=split,
        in_specs=(
            P(GROUP + FSDP, None),
            P(GROUP + FSDP, cols),
            P(rows, cols),
            P(rows, cols),
            P(rows, cols),
            P(None, GROUP, FSDP + (YL,)),
            P(None, ALL, None),
            P(None, ALL, None),
            P(ALL, None, None),
            P(ALL, None, None),
            P(ALL),
        ),
        out_specs=(P(rows, cols), P(rows, cols), P(rows, cols), P(None, ALL, None)),
        check_vma=False,
    )
```

time: 178 us -> 167 us (0.938)
  the two profiles are of different devices: /device:TPU:2 before, /device:TPU:9 now
where the time goes in v3:
time: 167 us; the launch traced here: 166 us
  starting transfers between devices  67.8 us (41%)
  waiting for transfers between devices  49.9 us (30%)
  Pallas kernels  19.8 us (12%)
  local copies, waits for them, and re-layouts  16.8 us (10%)
  matrix products  5.52 us (3%)
  other arithmetic  5.45 us (3%)
    all_to_all x1, starting transfers between devices, per_device(): parts = lax.all_to_all(parts, (GZ, YH), 0, 0, tiled=True)  18.5 us
    ppermute x1, waiting for transfers between devices, per_device(): near = lax.ppermute(hidden, YL, [(0, 1), (1, 0), (2, 3), (3, 2)])  15.5 us
    all_to_all x1, waiting for transfers between devices, per_device(): parts = lax.all_to_all(parts, (GZ, YH), 0, 0, tiled=True)  12.5 us
    all_to_all x1, waiting for transfers between devices, per_device(): parts = lax.all_to_all(parts, GX, 0, 0, tiled=True)  10.2 us
    all_to_all x1, starting transfers between devices, per_device(): both = lax.all_to_all(both, GROUP, 0, 0, tiled=True)  9.13 us
    all_to_all x1, starting transfers between devices, per_device(): values = lax.all_to_all(values, (YH, CO, YL), 0, 0, tiled=True)  8.53 us
    all_to_all x1, waiting for transfers between devices, per_device(): values = lax.all_to_all(values, (YH, CO, YL), 0, 0, tiled=True)  6.49 us
    broadcast_in_dim x6, local copies, waits for them, and re-layouts, spread_probs(): spread = jnp.where(same, spread, jnp.zeros((), jnp.bfloat16))  6.17 us
  transfers between devices with their start and end apart: 12, of which 7 were waited for; matrix products, arithmetic and copies ran while one was open for 13% of the time, Pallas kernels for 6%

profile of v3, /device:TPU:9, one launch (start us, length us, event | category | flops | bytes accessed | tf_op | source)
XLA Modules:
  0.0 166.2 jit_solution(13810340894093422481)
XLA Ops:
  0.6 2.6 %collective-permute-start = (bf16[128,8192]{1,0:T(8,128)(2,1)}, bf16[128,8192]{1,0:T(8,128)(2,1)S(1)}, u32[]{:S(2)}, u32[]{:S(2)}) collective-permute-start(bf16[128,8192]{1,0:T(8,128)(2,1)} %own_1.1), channel_id=1, source_target_pairs={{0,4},{4,0},{1,5},{5,1},{2,6},{6,2},{3,7},{7,3},{8,12},{12,8},{9,1... | collective-permute-start | bytes 6291464 | tf_op jit(solution)/shard_map/ppermute | solution.py:296
  3.2 4.2 %collective-permute-start.1 = (bf16[128,128]{1,0:T(8,128)(2,1)}, bf16[128,128]{1,0:T(8,128)(2,1)S(1)}, u32[]{:S(2)}, u32[]{:S(2)}) collective-permute-start(bf16[128,128]{1,0:T(8,128)(2,1)} %param.12), channel_id=1, source_target_pairs={{0,0},{1,1},{2,2},{3,3},{6,4},{7,5},{4,6},{5,7},{8,8},{9,9},{10,10... | collective-permute-start | bytes 98312 | tf_op jit(solution)/shard_map/ppermute | solution.py:295
  7.4 1.9 %collective-permute-start.2 = (bf16[128,128]{1,0:T(8,128)(2,1)}, bf16[128,128]{1,0:T(8,128)(2,1)S(1)}, u32[]{:S(2)}, u32[]{:S(2)}) collective-permute-start(bf16[128,128]{1,0:T(8,128)(2,1)} %param.12), channel_id=1, source_target_pairs={{4,0},{5,1},{6,2},{7,3},{2,4},{3,5},{0,6},{1,7},{12,8},{13,9},{14,... | collective-permute-start | bytes 98312 | tf_op jit(solution)/shard_map/ppermute | solution.py:295
  10.9 2.0 %collective-permute-start.3 = (f32[3,48,128]{2,1,0:T(8,128)S(1)}, f32[3,48,128]{2,1,0:T(8,128)S(1)}, u32[]{:S(2)}, u32[]{:S(2)}) collective-permute-start(f32[3,48,128]{2,1,0:T(8,128)S(1)} %pad_maximum_fusion), channel_id=1, source_target_pairs={{0,0},{1,1},{2,2},{3,3},{6,4},{7,5},{4,6},{5,7},{16,16},{17,17},{1... | collective-permute-start | bytes 221192 | tf_op jit(solution)/shard_map/ppermute | solution.py:314
  15.1 3.1 %partial_gradient.1 = bf16[4,2,512,128]{3,2,1,0:T(8,128)(2,1)} custom-call(s32[1]{0:T(128)} %bitcast.t, s32[1]{0:T(128)} %bitcast.1.core, bf16[128,8192]{1,0:T(8,128)(2,1)} %own_1.1, bf16[128,8192]{1,0:T(8,128)(2,1)} %own_1.1, bf16[128,8192]{1,0:T(8,128)(2,1)} %copy-done.1, bf16[128,8192]{1,0:T(8,128)(2,1)} %copy-done.1, bf16[128,128]{1,0:T(8,128)(2,1)} %copy-done.11, ...), custom_call_target="tpu_custom_call" | custom-call | tf_op jit(solution)/shard_map/partial_gradient/pallas_call | solution.py:64
  18.2 4.2 %all-to-all-start = ((bf16[4,2,512,128]{3,2,1,0:T(8,128)(2,1)}), bf16[4,2,512,128]{3,2,1,0:T(8,128)(2,1)S(1)}, u32[]{:S(2)}, u32[]{:S(2)}) async-start(bf16[4,2,512,128]{3,2,1,0:T(8,128)(2,1)} %partial_gradient.1), calls=%async_computation | async-start | bytes 2097152 | tf_op jit(solution)/shard_map/all_to_all | solution.py:301
  23.5 2.5 %fusion.13 = (f32[16,4,8,4]{2,3,1,0:T(4,128)S(1)}, f32[16,4,8,4,4]{2,4,3,1,0:T(4,128)S(1)}) fusion(bf16[4,16,4,8,128]{4,3,2,1,0:T(8,128)(2,1)S(1)} %bitcast.42, bf16[4,16,4,128,1]{3,2,1,0,4:T(4,128)(2,1)S(1)} %bitcast.46, pred[4,4]{1,0:T(4,128)(4,1)S(1)} %iota_compare_fusion.2), kind=kOutput, calls=%fused_computation.29 | convolution fusion | flops 2119680 | bytes 630800 | tf_op jit(solution)/shard_map/tnhjd,snhd->nhjts/dot_general | solution.py:204
  26.0 1.6 fusion.12
  27.6 10.2 %all-to-all-done.parts = bf16[4,2,512,128]{3,2,1,0:T(8,128)(2,1)S(1)} async-done(((bf16[4,2,512,128]{3,2,1,0:T(8,128)(2,1)}), bf16[4,2,512,128]{3,2,1,0:T(8,128)(2,1)S(1)}, u32[]{:S(2)}, u32[]{:S(2)}) %all-to-all-start) | async-done | bytes 1048608 | tf_op jit(solution)/shard_map/all_to_all | solution.py:301
  38.7 2.1 %sum_over_x.1 = bf16[12,2,48,128]{3,2,1,0:T(8,128)(2,1)} custom-call(bf16[4,2,512,128]{3,2,1,0:T(8,128)(2,1)} %copy-done.3), custom_call_target="tpu_custom_call" | custom-call | tf_op jit(solution)/shard_map/sum_over_x/pallas_call | solution.py:95
  40.8 18.5 %all-to-all-start.1 = ((bf16[24,48,128]{2,1,0:T(8,128)(2,1)}), bf16[24,48,128]{2,1,0:T(8,128)(2,1)S(1)}, u32[]{:S(2)}, u32[]{:S(2)}) async-start(bf16[24,48,128]{2,1,0:T(8,128)(2,1)} %bitcast.39), calls=%async_computation.1 | async-start | bytes 589824 | tf_op jit(solution)/shard_map/all_to_all | solution.py:317
  60.6 1.4 divide_convert_fusion
  62.4 12.5 %all-to-all-done.1.parts = bf16[24,48,128]{2,1,0:T(8,128)(2,1)S(1)} async-done(((bf16[24,48,128]{2,1,0:T(8,128)(2,1)}), bf16[24,48,128]{2,1,0:T(8,128)(2,1)S(1)}, u32[]{:S(2)}, u32[]{:S(2)}) %all-to-all-start.1) | async-done | bytes 294944 | tf_op jit(solution)/shard_map/all_to_all | solution.py:317
  75.6 1.6 update_shard.1
  77.2 2.4 %collective-permute-start.4 = (bf16[48,128]{1,0:T(8,128)(2,1)}, bf16[48,128]{1,0:T(8,128)(2,1)S(1)}, u32[]{:S(2)}, u32[]{:S(2)}) collective-permute-start(bf16[48,128]{1,0:T(8,128)(2,1)} %get-tuple-element.27), channel_id=1, source_target_pairs={{0,0},{1,1},{2,2},{3,3},{4,6},{5,7},{6,4},{7,5},{16,16},{17,17},{1... | collective-permute-start | bytes 36872 | tf_op jit(solution)/shard_map/ppermute | solution.py:322
  79.6 3.1 %collective-permute-done.4 = bf16[48,128]{1,0:T(8,128)(2,1)S(1)} collective-permute-done((bf16[48,128]{1,0:T(8,128)(2,1)}, bf16[48,128]{1,0:T(8,128)(2,1)S(1)}, u32[]{:S(2)}, u32[]{:S(2)}) %collective-permute-start.4) | collective-permute-done | bytes 12320 | tf_op jit(solution)/shard_map/ppermute | solution.py:322
  83.5 1.2 broadcast_in_dim.71
  84.7 9.1 %all-to-all-start.2 = ((bf16[48,2,48,128]{3,2,1,0:T(8,128)(2,1)}), bf16[48,2,48,128]{3,2,1,0:T(8,128)(2,1)S(1)}, u32[]{:S(2)}, u32[]{:S(2)}) async-start(bf16[48,2,48,128]{3,2,1,0:T(8,128)(2,1)} %broadcast_in_dim.71), calls=%async_computation.2 | async-start | bytes 2359296 | tf_op jit(solution)/shard_map/all_to_all | solution.py:324
  93.8 3.0 %collective-permute-start.5 = (bf16[4,256,512]{2,1,0:T(8,128)(2,1)}, bf16[4,256,512]{2,1,0:T(8,128)(2,1)}, u32[]{:S(2)}, u32[]{:S(2)}) collective-permute-start(bf16[4,256,512]{2,1,0:T(8,128)(2,1)} %own.1), channel_id=1, source_target_pairs={{0,1},{1,0},{2,3},{3,2},{4,5},{5,4},{6,7},{7,6},{8,9},{9,8},{10,11... | collective-permute-start | bytes 3145736 | tf_op jit(solution)/shard_map/ppermute | solution.py:302
  96.8 5.3 %collective-permute-start.6 = (bf16[4,256,512]{2,1,0:T(8,128)(2,1)}, bf16[4,256,512]{2,1,0:T(8,128)(2,1)}, u32[]{:S(2)}, u32[]{:S(2)}) collective-permute-start(bf16[4,256,512]{2,1,0:T(8,128)(2,1)} %own.1), channel_id=1, source_target_pairs={{0,4},{4,0},{1,5},{5,1},{2,6},{6,2},{3,7},{7,3},{8,12},{12,8},{9,1... | collective-permute-start | bytes 3145736 | tf_op jit(solution)/shard_map/ppermute | solution.py:326
  102.1 15.5 %collective-permute-done.5.near = bf16[4,256,512]{2,1,0:T(8,128)(2,1)} collective-permute-done((bf16[4,256,512]{2,1,0:T(8,128)(2,1)}, bf16[4,256,512]{2,1,0:T(8,128)(2,1)}, u32[]{:S(2)}, u32[]{:S(2)}) %collective-permute-start.5) | collective-permute-done | bytes 1048608 | tf_op jit(solution)/shard_map/ppermute | solution.py:302
  117.6 6.1 %collective-permute-start.7 = (bf16[4,256,512]{2,1,0:T(8,128)(2,1)}, bf16[4,256,512]{2,1,0:T(8,128)(2,1)}, u32[]{:S(2)}, u32[]{:S(2)}) collective-permute-start(bf16[4,256,512]{2,1,0:T(8,128)(2,1)} %collective-permute-done.5.near), channel_id=1, source_target_pairs={{0,4},{4,0},{1,5},{5,1},{2,6},{6,2},{3,7},{7,3},{8,12},{12,8},{9,1... | collective-permute-start | bytes 3145736 | tf_op jit(solution)/shard_map/ppermute | solution.py:327
  127.3 3.6 %broadcast_in_dim.76 = bf16[4,512,64]{1,2,0:T(8,128)(2,1)S(1)} reshape(bf16[4,8,4,16,4,16]{3,2,1,5,4,0:T(4,128)(2,1)S(1)} %broadcast_in_dim.75) | data formatting | bytes 524288 | tf_op jit(solution)/shard_map/jit(_where)/broadcast_in_dim | solution.py:230
  131.2 1.5 convolution_bitcast_fusion
  132.7 1.6 copy.29
  135.1 1.3 all-to-all-done.2
  136.4 1.0 copy-done
  137.4 4.9 %values_part.1 = bf16[16,64,128]{2,1,0:T(8,128)(2,1)} custom-call(bf16[12,4,2,48,128]{4,3,2,1,0:T(8,128)(2,1)} %bitcast.35, bf16[4,256,512]{2,1,0:T(8,128)(2,1)} %own.1, bf16[4,256,512]{2,1,0:T(8,128)(2,1)} %collective-permute-done.5.near, bf16[4,256,512]{2,1,0:T(8,128)(2,1)} %collective-permute-done.6.far_own, ...), custom_call_target="tpu_custom_call" | custom-call | tf_op jit(solution)/shard_map/values_part/pallas_call | solution.py:175
  142.3 8.5 %all-to-all-start.3 = ((bf16[16,64,128]{2,1,0:T(8,128)(2,1)}), bf16[16,64,128]{2,1,0:T(8,128)(2,1)S(1)}, u32[]{:S(2)}, u32[]{:S(2)}) async-start(bf16[16,64,128]{2,1,0:T(8,128)(2,1)} %values_part.1), calls=%async_computation.3 | async-start | bytes 524288 | tf_op jit(solution)/shard_map/all_to_all | solution.py:334
  150.8 4.3 %update_all.1 = (bf16[2048,128]{1,0:T(8,128)(2,1)}, f32[2048,128]{1,0:T(8,128)}, f32[2048,128]{1,0:T(8,128)}) custom-call(s32[1]{0:T(128)} %bitcast.t, s32[1]{0:T(128)} %bitcast.1.core, bf16[12,4,2,48,128]{4,3,2,1,0:T(8,128)(2,1)} %bitcast.36, bf16[2048,128]{1,0:T(8,128)(2,1)} %weight.1, f32[2048,128]{1,0:T(8,128)} %one.1, f32[2048,128]{1,0:T(8,128)} %two.1), custom_call_target="tpu_custom_call" | custom-call | tf_op jit(solution)/shard_map/update_all/pallas_call | solution.py:143
  155.2 6.5 %all-to-all-done.3.first_0.first_1.second_0.second_1 = bf16[16,64,128]{2,1,0:T(8,128)(2,1)S(1)} async-done(((bf16[16,64,128]{2,1,0:T(8,128)(2,1)}), bf16[16,64,128]{2,1,0:T(8,128)(2,1)S(1)}, u32[]{:S(2)}, u32[]{:S(2)}) %all-to-all-start.3) | async-done | bytes 262176 | tf_op jit(solution)/shard_map/all_to_all | solution.py:334
  162.4 3.8 %finish_attention.1 = bf16[64,4096]{1,0:T(8,128)(2,1)} custom-call(bf16[16,64,128]{2,1,0:T(8,128)(2,1)} %copy-done.2, bf16[16,64,128]{2,1,0:T(8,128)(2,1)} %copy-done.2, bf16[16,64,128]{2,1,0:T(8,128)(2,1)} %copy-done.2, bf16[16,64,128]{2,1,0:T(8,128)(2,1)} %copy-done.2, f32[4,512,128]{2,1,0:T(8,128)} %bitcast.37, ...), custom_call_target="tpu_custom_call" | custom-call | tf_op jit(solution)/shard_map/finish_attention/pallas_call | solution.py:258
  (56 shorter events, 14.3 us)
Async XLA Ops:
  0.6 13.2 %collective-permute-start = (bf16[128,8192]{1,0:T(8,128)(2,1)}, bf16[128,8192]{1,0:T(8,128)(2,1)S(1)}, u32[]{:S(2)}, u32[]{:S(2)}) collective-permute-start(bf16[128,8192]{1,0:T(8,128)(2,1)} %own_1.1), channel_id=1, source_target_pairs={{0,4},{4,0},{1,5},{5,1},{2,6},{6,2},{3,7},{7,3},{8,12},{12,8},{9,1... | collective-permute-start | bytes 6291464 | tf_op jit(solution)/shard_map/ppermute | solution.py:296
  3.2 9.7 %collective-permute-start.1 = (bf16[128,128]{1,0:T(8,128)(2,1)}, bf16[128,128]{1,0:T(8,128)(2,1)S(1)}, u32[]{:S(2)}, u32[]{:S(2)}) collective-permute-start(bf16[128,128]{1,0:T(8,128)(2,1)} %param.12), channel_id=1, source_target_pairs={{0,0},{1,1},{2,2},{3,3},{6,4},{7,5},{4,6},{5,7},{8,8},{9,9},{10,10... | collective-permute-start | bytes 98312 | tf_op jit(solution)/shard_map/ppermute | solution.py:295
  7.4 6.3 %collective-permute-start.2 = (bf16[128,128]{1,0:T(8,128)(2,1)}, bf16[128,128]{1,0:T(8,128)(2,1)S(1)}, u32[]{:S(2)}, u32[]{:S(2)}) collective-permute-start(bf16[128,128]{1,0:T(8,128)(2,1)} %param.12), channel_id=1, source_target_pairs={{4,0},{5,1},{6,2},{7,3},{2,4},{3,5},{0,6},{1,7},{12,8},{13,9},{14,... | collective-permute-start | bytes 98312 | tf_op jit(solution)/shard_map/ppermute | solution.py:295
  10.9 51.4 %collective-permute-start.3 = (f32[3,48,128]{2,1,0:T(8,128)S(1)}, f32[3,48,128]{2,1,0:T(8,128)S(1)}, u32[]{:S(2)}, u32[]{:S(2)}) collective-permute-start(f32[3,48,128]{2,1,0:T(8,128)S(1)} %pad_maximum_fusion), channel_id=1, source_target_pairs={{0,0},{1,1},{2,2},{3,3},{6,4},{7,5},{4,6},{5,7},{16,16},{17,17},{1... | collective-permute-start | bytes 221192 | tf_op jit(solution)/shard_map/ppermute | solution.py:314
  12.9 0.9 copy-start.11
  13.8 0.6 copy-start.12
  13.8 1.3 copy-start.1
  18.2 4.2 %copy-start.13 = (s32[16]{0:T(128)S(1)}, s32[16]{0:T(128)}, u32[]{:S(2)}) copy-start(s32[16]{0:T(128)} %param.21) | copy-start | bytes 196
  18.2 4.3 %copy-start.5 = (bf16[4,16,4096]{2,1,0:T(8,128)(2,1)S(1)}, bf16[4,16,4096]{2,1,0:T(8,128)(2,1)}, u32[]{:S(2)}) copy-start(bf16[4,16,4096]{2,1,0:T(8,128)(2,1)} %param.17) | copy-start | bytes 1572868
  18.2 4.4 %copy-start.10 = (bf16[4,16,512]{2,1,0:T(8,128)(2,1)S(1)}, bf16[4,16,512]{2,1,0:T(8,128)(2,1)}, u32[]{:S(2)}) copy-start(bf16[4,16,512]{2,1,0:T(8,128)(2,1)} %param.18) | copy-start | bytes 196612
  18.2 4.4 %copy-start.6 = (bf16[16,32,512]{2,1,0:T(8,128)(2,1)S(1)}, bf16[16,32,512]{2,1,0:T(8,128)(2,1)}, u32[]{:S(2)}) copy-start(bf16[16,32,512]{2,1,0:T(8,128)(2,1)} %param.19) | copy-start | bytes 1572868
  18.2 19.5 %all-to-all-start = ((bf16[4,2,512,128]{3,2,1,0:T(8,128)(2,1)}), bf16[4,2,512,128]{3,2,1,0:T(8,128)(2,1)S(1)}, u32[]{:S(2)}, u32[]{:S(2)}) async-start(bf16[4,2,512,128]{3,2,1,0:T(8,128)(2,1)} %partial_gradient.1), calls=%async_computation | async-start | bytes 2097152 | tf_op jit(solution)/shard_map/all_to_all | solution.py:301
  37.7 1.0 copy-start.3
  40.8 34.1 %all-to-all-start.1 = ((bf16[24,48,128]{2,1,0:T(8,128)(2,1)}), bf16[24,48,128]{2,1,0:T(8,128)(2,1)S(1)}, u32[]{:S(2)}, u32[]{:S(2)}) async-start(bf16[24,48,128]{2,1,0:T(8,128)(2,1)} %bitcast.39), calls=%async_computation.1 | async-start | bytes 589824 | tf_op jit(solution)/shard_map/all_to_all | solution.py:317
  62.4 12.5 %copy-start.9 = (f32[3,48,128]{2,1,0:T(8,128)}, f32[3,48,128]{2,1,0:T(8,128)S(1)}, u32[]{:S(2)}) copy-start(f32[3,48,128]{2,1,0:T(8,128)S(1)} %collective-permute-done.3.state) | copy-start | bytes 221188
  74.9 0.7 copy-start.4
  77.2 5.6 %collective-permute-start.4 = (bf16[48,128]{1,0:T(8,128)(2,1)}, bf16[48,128]{1,0:T(8,128)(2,1)S(1)}, u32[]{:S(2)}, u32[]{:S(2)}) collective-permute-start(bf16[48,128]{1,0:T(8,128)(2,1)} %get-tuple-element.27), channel_id=1, source_target_pairs={{0,0},{1,1},{2,2},{3,3},{4,6},{5,7},{6,4},{7,5},{16,16},{17,17},{1... | collective-permute-start | bytes 36872 | tf_op jit(solution)/shard_map/ppermute | solution.py:322
  83.5 41.9 %copy-start.7 = (bf16[16,32,512]{2,1,0:T(8,128)(2,1)S(1)}, bf16[16,32,512]{2,1,0:T(8,128)(2,1)}, u32[]{:S(2)}) copy-start(bf16[16,32,512]{2,1,0:T(8,128)(2,1)} %param.20) | copy-start | bytes 1572868
  84.7 51.7 %all-to-all-start.2 = ((bf16[48,2,48,128]{3,2,1,0:T(8,128)(2,1)}), bf16[48,2,48,128]{3,2,1,0:T(8,128)(2,1)S(1)}, u32[]{:S(2)}, u32[]{:S(2)}) async-start(bf16[48,2,48,128]{3,2,1,0:T(8,128)(2,1)} %broadcast_in_dim.71), calls=%async_computation.2 | async-start | bytes 2359296 | tf_op jit(solution)/shard_map/all_to_all | solution.py:324
  93.8 23.8 %collective-permute-start.5 = (bf16[4,256,512]{2,1,0:T(8,128)(2,1)}, bf16[4,256,512]{2,1,0:T(8,128)(2,1)}, u32[]{:S(2)}, u32[]{:S(2)}) collective-permute-start(bf16[4,256,512]{2,1,0:T(8,128)(2,1)} %own.1), channel_id=1, source_target_pairs={{0,1},{1,0},{2,3},{3,2},{4,5},{5,4},{6,7},{7,6},{8,9},{9,8},{10,11... | collective-permute-start | bytes 3145736 | tf_op jit(solution)/shard_map/ppermute | solution.py:302
  96.8 39.6 %collective-permute-start.6 = (bf16[4,256,512]{2,1,0:T(8,128)(2,1)}, bf16[4,256,512]{2,1,0:T(8,128)(2,1)}, u32[]{:S(2)}, u32[]{:S(2)}) collective-permute-start(bf16[4,256,512]{2,1,0:T(8,128)(2,1)} %own.1), channel_id=1, source_target_pairs={{0,4},{4,0},{1,5},{5,1},{2,6},{6,2},{3,7},{7,3},{8,12},{12,8},{9,1... | collective-permute-start | bytes 3145736 | tf_op jit(solution)/shard_map/ppermute | solution.py:326
  117.6 18.8 %collective-permute-start.7 = (bf16[4,256,512]{2,1,0:T(8,128)(2,1)}, bf16[4,256,512]{2,1,0:T(8,128)(2,1)}, u32[]{:S(2)}, u32[]{:S(2)}) collective-permute-start(bf16[4,256,512]{2,1,0:T(8,128)(2,1)} %collective-permute-done.5.near), channel_id=1, source_target_pairs={{0,4},{4,0},{1,5},{5,1},{2,6},{6,2},{3,7},{7,3},{8,12},{12,8},{9,1... | collective-permute-start | bytes 3145736 | tf_op jit(solution)/shard_map/ppermute | solution.py:327
  131.2 3.1 %copy-start.8 = (pred[512,64]{1,0:T(8,128)(4,1)S(1)}, pred[512,64]{1,0:T(8,128)(4,1)}, u32[]{:S(2)}) copy-start(pred[512,64]{1,0:T(8,128)(4,1)} %copy.30) | copy-start | bytes 98308
  136.4 1.0 copy-start
  142.3 19.4 %all-to-all-start.3 = ((bf16[16,64,128]{2,1,0:T(8,128)(2,1)}), bf16[16,64,128]{2,1,0:T(8,128)(2,1)S(1)}, u32[]{:S(2)}, u32[]{:S(2)}) async-start(bf16[16,64,128]{2,1,0:T(8,128)(2,1)} %values_part.1), calls=%async_computation.3 | async-start | bytes 524288 | tf_op jit(solution)/shard_map/all_to_all | solution.py:334
  161.7 0.7 copy-start.2
